TPU v7x, 16 devices: a 4x2x1 block of a 4x4x8 slice. The times are simulated.
16 devices in a mesh: dp: 2 (over y, z), ep: 8 (over x, core).
Axes of the slice: x: 4, y: 2, z: 1, core: 2. Of those that a mesh axis runs over, the one named last changes fastest.
The devices are a block of a 4x4x8 slice.
Arguments:
- tokens: bfloat16 [65536, 768], P(('dp', 'ep')), parts along dimension 0
- topk_idx: int32 [65536, 1], P(('dp', 'ep')), parts along dimension 0
- topk_w: float32 [65536, 1], P(('dp', 'ep')), parts along dimension 0
- w_up: bfloat16 [8, 17, 768, 3072], P('ep')
- w_down: bfloat16 [8, 17, 3072, 768], P('ep')
- slot_expert: int32 [8, 17], replicated
Outputs:
- output: bfloat16 [65536, 768], P(('dp', 'ep')), parts along dimension 0
There are 2 independent parts. A program takes and returns all parts, laid end to end along the dimension named above; an argument that names none is the same for every part.
All inputs are finite; a program needn't handle non-finite values.
Results may differ from a plain program's by a relative error of at most 0.001.
Values are sent between devices in bfloat16 or wider.
A program may use at most 768 MiB of HBM per device.

v0:
```python
import jax
import jax.numpy as jnp
from jax import lax
from jax.sharding import PartitionSpec as P

MAX_COPIES = 4


def slot_bound(n_tok, n_top, n_dev, n_slot):
    base_load = (n_tok * n_top) // (n_dev * n_slot)
    return base_load + base_load // 2 + 1


def route_pairs(topk_idx, slot_expert, capacity):
    n_dev, n_slot = slot_expert.shape
    n_exp = n_dev * (n_slot - 1)
    n_top = topk_idx.shape[1]
    table_flat = slot_expert.reshape(-1)
    slot_ids = jnp.arange(n_dev * n_slot, dtype=jnp.int32)
    same_exp = table_flat[:, None] == table_flat[None, :]
    earlier = slot_ids[None, :] < slot_ids[:, None]
    copy_rank = jnp.sum(same_exp & earlier, axis=1, dtype=jnp.int32)
    exp_copies = jax.ops.segment_sum(jnp.ones_like(table_flat), table_flat, num_segments=n_exp)
    slot_of = jnp.zeros((n_exp, MAX_COPIES), jnp.int32).at[table_flat, copy_rank].set(slot_ids)
    flat_exp = topk_idx.reshape(-1)
    onehot = (flat_exp[:, None] == jnp.arange(n_exp, dtype=jnp.int32)[None, :]).astype(jnp.int32)
    pair_rank = jnp.sum((jnp.cumsum(onehot, axis=0) - onehot) * onehot, axis=1)
    pair_copies = exp_copies[flat_exp]
    slot_flat = slot_of[flat_exp, pair_rank % pair_copies]
    buf_row = pair_rank // pair_copies
    pair_pos = ((slot_flat % n_slot) * n_dev + slot_flat // n_slot) * capacity + buf_row
    pair_tok = jnp.arange(flat_exp.shape[0], dtype=jnp.int32) // n_top
    buf_tok = jnp.zeros((n_slot * n_dev * capacity,), jnp.int32).at[pair_pos].set(pair_tok)
    return pair_pos, buf_tok


def expert_ffn(recv_buf, up_local, down_local):
    pre_act = jnp.einsum('spcm,smf->spcf', recv_buf, up_local, preferred_element_type=jnp.float32)
    hidden = jax.nn.gelu(pre_act, approximate=True).astype(jnp.bfloat16)
    return jnp.einsum('spcf,sfm->spcm', hidden, down_local, preferred_element_type=jnp.float32).astype(jnp.bfloat16)


def solution(mesh):
    def group_layer(tokens, topk_idx, topk_w, w_up, w_down, slot_expert):
        n_tok, d_model = tokens.shape
        n_top = topk_idx.shape[1]
        n_dev, n_slot = slot_expert.shape
        capacity = slot_bound(n_tok, n_top, n_dev, n_slot)
        pair_pos, buf_tok = route_pairs(topk_idx, slot_expert, capacity)
        send_buf = tokens[buf_tok].reshape(n_slot, n_dev, capacity, d_model)
        recv_buf = lax.all_to_all(send_buf, 'ep', 1, 1, tiled=True)
        expert_out = expert_ffn(recv_buf, w_up[0], w_down[0])
        back_buf = lax.all_to_all(expert_out, 'ep', 1, 1, tiled=True)
        pair_out = back_buf.reshape(-1, d_model)[pair_pos].reshape(n_tok, n_top, d_model)
        mixed_out = jnp.sum(pair_out.astype(jnp.float32) * topk_w[:, :, None], axis=1)
        return mixed_out.astype(jnp.bfloat16)

    row_spec = P(('dp', 'ep'), None)
    weight_spec = P('ep', None, None, None)
    return jax.shard_map(group_layer, mesh=mesh, in_specs=(row_spec, row_spec, row_spec, weight_spec, weight_spec, P(None, None)), out_specs=row_spec, check_vma=False)
```

profile of v0, /device:TPU:113, one launch (start us, length us, event | category | flops | bytes accessed | tf_op | source)
XLA Modules:
  0.0 542.2 jit_solution(9279892939209652656)
XLA Ops:
  0.0 0.8 eq.53
  0.8 0.8 reshape.233
  1.5 0.2 convert_reduce_fusion
  1.7 0.7 compare_select_fusion.3
  2.5 0.8 copy.16
  3.3 0.6 fusion.20
  3.9 1.5 scatter_custom_fusion.1
  5.4 0.1 reduce-window.9
  5.5 0.2 broadcast_add_fusion
  5.7 0.0 copy-start
  5.7 1.2 copy.17
  7.0 24.7 %gather_fusion = s32[4096]{0:T(1024)S(1)} fusion(s32[128]{0:T(128)S(1)} %scatter_custom_fusion.1, s32[4096]{0:T(1024)S(1)} %broadcast_clamp_fusion.1), kind=kCustom, calls=%fused_computation | custom fusion | bytes 49152 | tf_op jit(solution)/shard_map/gather | solution.py:28
  31.7 0.0 copy-done
  31.7 1.4 fusion.19
  33.1 1.4 fusion.28
  34.6 7.1 %scatter_fusion = s32[128,4]{0,1:T(4,128)S(1)} fusion(s32[128,4]{0,1:T(4,128)S(1)} %broadcast_in_dim.14, s32[136]{0:T(256)S(1)} %bitcast.42, s32[136]{0:T(256)S(1)} %iota.20), kind=kCustom, calls=%fused_computation.4 | custom fusion | bytes 2720 | tf_op jit(solution)/shard_map/scatter | solution.py:24
  41.7 33.1 %gather_fusion.1 = s32[4096]{0:T(1024)S(1)} fusion(s32[128,4]{0,1:T(4,128)S(1)} %scatter_fusion, s32[4096]{0:T(1024)S(1)} %bitcast.41), kind=kCustom, calls=%fused_computation.1 | custom fusion | bytes 65536 | tf_op jit(solution)/shard_map/gather | solution.py:29
  74.8 1.4 compare_select_fusion
  76.3 0.0 copy-start.1
  76.3 15.7 %scatter_custom_fusion.2 = s32[6256]{0:T(1024)S(1)} fusion(s32[4096]{0:T(1024)S(1)} %bitcast.52, s32[4096]{0:T(1024)S(1)} %iota.21, s32[]{:T(128)} %constant.29.clone.1), kind=kCustom, calls=%fused_computation.52 | custom fusion | bytes 25028 | tf_op jit(solution)/shard_map/scatter | solution.py:33
  92.1 27.4 %gather_fusion.2 = bf16[6256,768]{1,0:T(8,128)(2,1)} fusion(bf16[4096,768]{1,0:T(8,128)(2,1)} %param.6, s32[7168]{0:T(1024)S(1)} %pad_clamp_fusion), kind=kCustom, calls=%fused_computation.2 | custom fusion | bytes 19243456 | tf_op jit(solution)/shard_map/gather | solution.py:50
  119.5 0.0 copy-done.1
  119.5 13.9 %reshape.235 = bf16[17,8,46,768]{3,2,1,0:T(8,128)(2,1)} reshape(bf16[6256,768]{1,0:T(8,128)(2,1)} %gather_fusion.2) | data formatting | bytes 19218432 | tf_op jit(solution)/shard_map/reshape | solution.py:50
  133.4 8.3 %copy.18 = bf16[17,8,46,768]{3,2,0,1:T(8,128)(2,1)} copy(bf16[17,8,46,768]{3,2,1,0:T(8,128)(2,1)} %reshape.235) | data formatting | bytes 19218432 | tf_op jit(solution)/shard_map/reshape | solution.py:50
  141.7 118.4 %all_to_all.10 = bf16[17,8,46,768]{3,2,0,1:T(8,128)(2,1)} all-to-all(bf16[17,8,46,768]{3,2,0,1:T(8,128)(2,1)} %copy.18), channel_id=1, replica_groups=mesh['dp'=2,'ep'=8] {'ep'}, dimensions={1} | all-to-all | bytes 19218432 | tf_op jit(solution)/shard_map/all_to_all | solution.py:51
  260.1 54.2 %fusion.7 = bf16[17,8,46,3072]{3,2,1,0:T(8,128)(2,1)} fusion(bf16[1,17,768,3072]{3,2,1,0:T(8,128)(2,1)} %param.9, bf16[17,8,46,768]{3,2,0,1:T(8,128)(2,1)} %all_to_all.10), kind=kOutput, calls=%fused_computation.15 | convolution fusion | flops 29692477440 | bytes 128262144 | tf_op jit(solution)/shard_map/spcm,smf->spcf/dot_general | solution.py:38
  314.3 48.5 %fusion.15 = bf16[17,8,46,768]{3,2,1,0:T(8,128)(2,1)} fusion(bf16[17,8,46,3072]{3,2,1,0:T(8,128)(2,1)} %fusion.7, bf16[1,17,3072,768]{3,2,1,0:T(8,128)(2,1)} %param.10), kind=kOutput, calls=%fused_computation.22 | convolution fusion | flops 29524316160 | bytes 128262144 | tf_op jit(solution)/shard_map/spcf,sfm->spcm/dot_general | solution.py:40
  362.9 8.3 %copy.20 = bf16[17,8,46,768]{3,2,0,1:T(8,128)(2,1)} copy(bf16[17,8,46,768]{3,2,1,0:T(8,128)(2,1)} %fusion.15) | data formatting | bytes 19218432 | tf_op jit(solution)/shard_map/convert_element_type | solution.py:40
  371.2 0.0 copy-start.2
  371.2 5.8 %all-to-all-start.1 = ((bf16[17,8,46,768]{3,2,0,1:T(8,128)(2,1)}), bf16[17,8,46,768]{3,2,0,1:T(8,128)(2,1)}, u32[]{:S(2)}, u32[]{:S(2)}) async-start(bf16[17,8,46,768]{3,2,0,1:T(8,128)(2,1)} %copy.20), calls=%async_computation.1 | async-start | bytes 20054016 | tf_op jit(solution)/shard_map/all_to_all | solution.py:53
  377.0 0.0 copy-done.2
  377.0 111.2 %all-to-all-done.1 = bf16[17,8,46,768]{3,2,0,1:T(8,128)(2,1)} async-done(((bf16[17,8,46,768]{3,2,0,1:T(8,128)(2,1)}), bf16[17,8,46,768]{3,2,0,1:T(8,128)(2,1)}, u32[]{:S(2)}, u32[]{:S(2)}) %all-to-all-start.1) | async-done | bytes 9609248 | tf_op jit(solution)/shard_map/all_to_all | solution.py:53
  488.1 8.8 %copy.21 = bf16[17,8,46,768]{3,2,1,0:T(8,128)(2,1)} copy(bf16[17,8,46,768]{3,2,0,1:T(8,128)(2,1)} %all-to-all-done.1) | data formatting | bytes 19218432 | tf_op jit(solution)/shard_map/all_to_all | solution.py:53
  496.9 14.0 %reshape.236 = bf16[6256,768]{1,0:T(8,128)(2,1)} reshape(bf16[17,8,46,768]{3,2,1,0:T(8,128)(2,1)} %copy.21) | data formatting | bytes 19218432 | tf_op jit(solution)/shard_map/reshape | solution.py:54
  510.9 0.0 copy-start.3
  510.9 24.0 %gather_fusion.3 = bf16[4096,768]{1,0:T(8,128)(2,1)} fusion(bf16[6256,768]{1,0:T(8,128)(2,1)} %reshape.236, s32[4096]{0:T(1024)S(1)} %broadcast_clamp_fusion), kind=kCustom, calls=%fused_computation.3 | custom fusion | bytes 12599296 | tf_op jit(solution)/shard_map/gather | solution.py:54
  534.9 0.0 copy-done.3
  534.9 7.2 %multiply_convert_fusion = bf16[4096,768]{1,0:T(8,128)(2,1)} fusion(bf16[4096,768]{1,0:T(8,128)(2,1)} %gather_fusion.3, f32[4096]{0:T(1024)S(1)} %bitcast.54), kind=kLoop, calls=%fused_computation.20 | loop fusion | flops 9437184 | bytes 12599296 | tf_op jit(solution)/shard_map/convert_element_type | solution.py:56
  (13 shorter events, 0.1 us)
Async XLA Ops:
  5.7 26.0 %copy-start = (s32[4096,1]{0,1:T(1,128)S(1)}, s32[4096,1]{0,1:T(1,128)}, u32[]{:S(2)}) copy-start(s32[4096,1]{0,1:T(1,128)} %param.7) | copy-start | bytes 49156
  76.3 43.2 %copy-start.1 = (s32[4096,1]{0,1:T(1,128)}, s32[4096,1]{0,1:T(1,128)S(1)}, u32[]{:S(2)}) copy-start(s32[4096,1]{0,1:T(1,128)S(1)} %compare_select_fusion) | copy-start | bytes 49156
  371.2 5.8 %copy-start.2 = (s32[4096,1]{0,1:T(1,128)S(1)}, s32[4096,1]{0,1:T(1,128)}, u32[]{:S(2)}) copy-start(s32[4096,1]{0,1:T(1,128)} %copy-done.1) | copy-start | bytes 49156
  371.2 116.9 %all-to-all-start.1 = ((bf16[17,8,46,768]{3,2,0,1:T(8,128)(2,1)}), bf16[17,8,46,768]{3,2,0,1:T(8,128)(2,1)}, u32[]{:S(2)}, u32[]{:S(2)}) async-start(bf16[17,8,46,768]{3,2,0,1:T(8,128)(2,1)} %copy.20), calls=%async_computation.1 | async-start | bytes 20054016 | tf_op jit(solution)/shard_map/all_to_all | solution.py:53
  510.9 24.0 %copy-start.3 = (f32[4096,1]{0,1:T(1,128)S(1)}, f32[4096,1]{0,1:T(1,128)}, u32[]{:S(2)}) copy-start(f32[4096,1]{0,1:T(1,128)} %param.8) | copy-start | bytes 49156
where the time goes:
time: 544 us; the launch traced here: 542 us
  local copies, waits for them, and re-layouts  189 us (35%)
  blocking collectives  118 us (22%)
  waiting for transfers between devices  111 us (20%)
  matrix products  103 us (19%)
  other arithmetic  14.9 us (3%)
  starting transfers between devices  5.76 us (1%)
    all_to_all x1, blocking collectives, group_layer(): recv_buf = lax.all_to_all(send_buf, 'ep', 1, 1, tiled=True)  118 us
    all_to_all x1, waiting for transfers between devices, group_layer(): back_buf = lax.all_to_all(expert_out, 'ep', 1, 1, tiled=True)  111 us
    dot_general x1, matrix products, expert_ffn(): jnp.einsum('spcm,smf->spcf', recv_buf, up_local, preferred_element_type=j...  54.2 us
    dot_general x1, matrix products, expert_ffn(): jnp.einsum('spcf,sfm->spcm', hidden, down_local, preferred_element_type=j...  48.5 us
    gather x1, local copies, waits for them, and re-layouts, route_pairs(): slot_flat = slot_of[flat_exp, pair_rank % pair_copies]  33.1 us
    gather x1, local copies, waits for them, and re-layouts, group_layer(): send_buf = tokens[buf_tok].reshape(n_slot, n_dev, capacity, d_model)  27.4 us
    gather x1, local copies, waits for them, and re-layouts, route_pairs(): pair_copies = exp_copies[flat_exp]  24.7 us
    gather x1, local copies, waits for them, and re-layouts, group_layer(): back_buf.reshape(-1, d_model)[pair_pos].reshape(n_tok, n_top, d_model)  24 us
  transfers between devices with their start and end apart: 1, of which 1 were waited for; matrix products, arithmetic and copies ran while one was open for 0% of the time, Pallas kernels for 0%

commit v1 on v0

v1 whole, which is shorter than its diff:
```python
import functools
import math

import jax
import jax.numpy as jnp
from jax import lax
from jax.experimental import pallas as pl
from jax.experimental.pallas import tpu as pltpu
from jax.sharding import PartitionSpec as P

MESH = pl.DeviceIdType.MESH
LANES = 128
SUB = 8
PACK = 16
USTRIDE = 32
WIN = 64


def div_small(x, c):
    third = lax.shift_right_logical(x * 171, 9)
    quarter = lax.shift_right_logical(x, 2)
    half = lax.shift_right_logical(x, 1)
    return jnp.where(c == 1, x, jnp.where(c == 2, half, jnp.where(c == 3, third, quarter)))


def up_to(x, m):
    return -(-x // m) * m


def group_barrier(n_dev, me):
    barrier = pltpu.get_barrier_semaphore()
    for k in range(1, n_dev):
        pl.semaphore_signal(barrier, inc=1, device_id={'ep': lax.rem(me + k, n_dev)}, device_id_type=MESH)
    pl.semaphore_wait(barrier, n_dev - 1)


def route_kernel(n_dev, n_slot, stride, lo_bound, hi_bound, idx, table, addr, meta, flag, hsend, hall, tabcol, ssem, rsem):
    me = lax.axis_index('ep')
    f32, bf16, i32 = jnp.float32, jnp.bfloat16, jnp.int32
    n_rows = idx.shape[0]
    n_units = n_dev * USTRIDE
    group_barrier(n_dev, me)
    sub_e = lax.broadcasted_iota(i32, (LANES, LANES), 0)
    lane_e = lax.broadcasted_iota(i32, (LANES, LANES), 1)

    def count_row(r, acc):
        return acc + (sub_e == idx[pl.ds(r, 1), :]).astype(f32)

    seen = lax.fori_loop(0, n_rows, count_row, jnp.zeros((LANES, LANES), f32))
    hist = lax.dot_general(jnp.ones((SUB, LANES), bf16), seen.astype(bf16), (((1,), (1,)), ((), ())), preferred_element_type=f32)
    hsend[...] = hist.astype(i32)
    hall[me] = hist.astype(i32)
    sends = []
    for k in range(1, n_dev):
        copy = pltpu.make_async_remote_copy(src_ref=hsend, dst_ref=hall.at[me], send_sem=ssem.at[k], recv_sem=rsem.at[k], device_id={'ep': lax.rem(me + k, n_dev)}, device_id_type=MESH)
        copy.start()
        sends.append(copy)

    lane_u = lax.broadcasted_iota(i32, (1, n_units), 1)
    tabrow = jnp.full((1, n_units), -1, i32)
    tabcol[...] = jnp.full(tabcol.shape, -1, i32)
    for d in range(n_dev):
        for s in range(n_slot):
            u = d * USTRIDE + s
            tabrow = jnp.where(lane_u == u, table[d, s], tabrow)
            tabcol[u:u + 1, :] = jnp.full((1, LANES), table[d, s], i32)
    tcol = tabcol[...]
    unit_exp = (tcol == lax.broadcasted_iota(i32, (n_units, LANES), 1)).astype(bf16)
    same = jnp.concatenate([tcol] * (n_units // LANES), axis=1) == tabrow
    su = lax.broadcasted_iota(i32, (n_units, n_units), 0)
    lu = lax.broadcasted_iota(i32, (n_units, n_units), 1)
    copy_rank = jnp.sum(jnp.where(same & (su < lu), 1.0, 0.0), axis=0, keepdims=True).astype(i32)
    copies = jnp.sum(jnp.where(same, 1.0, 0.0), axis=0, keepdims=True).astype(i32)
    valid = tabrow >= 0
    before = ((su < lu) & (lax.shift_right_logical(su, 5) == lax.shift_right_logical(lu, 5))).astype(bf16)

    def slot_loads(h):
        per_unit = lax.dot_general(h.astype(bf16), unit_exp, (((1,), (1,)), ((), ())), preferred_element_type=f32).astype(i32)
        loads = jnp.where(valid, div_small(per_unit - copy_rank + copies - 1, copies), 0)
        starts = jnp.dot(loads.astype(bf16), before, preferred_element_type=f32).astype(i32)
        return loads, starts

    _, own_starts = slot_loads(hist)
    block = lax.rem(lax.shift_right_logical(lane_u, 5) + n_dev - me, n_dev)
    first = jnp.concatenate([own_starts, own_starts], axis=0) + block * stride
    row16 = lax.broadcasted_iota(i32, (2 * SUB, n_units), 0)
    part = jnp.where(row16 < 4, lax.shift_right_logical(first, 6), jnp.where(row16 < 8, first & 63, copies))
    chosen = (copy_rank == (row16 & 3)) & valid & (row16 < 9)
    exp_tab = jnp.dot(jnp.where(chosen, part, 0).astype(bf16), unit_exp, preferred_element_type=f32).astype(bf16)
    tri = (sub_e < lane_e).astype(bf16)
    ones = jnp.ones((LANES, LANES), bf16)

    def place_row(r, run):
        hot = sub_e == idx[pl.ds(r, 1), :]
        hot_b = hot.astype(bf16)
        prefix = jnp.dot(hot_b, tri, preferred_element_type=f32) + run
        rank = jnp.sum(jnp.where(hot, prefix, 0.0), axis=0, keepdims=True).astype(i32)
        got = jnp.dot(exp_tab, hot_b, preferred_element_type=f32).astype(i32)
        c = got[8:9]
        quot = div_small(rank, c)
        kk = rank - quot * c
        hi = jnp.where(kk == 0, got[0:1], jnp.where(kk == 1, got[1:2], jnp.where(kk == 2, got[2:3], got[3:4])))
        lo = jnp.where(kk == 0, got[4:5], jnp.where(kk == 1, got[5:6], jnp.where(kk == 2, got[6:7], got[7:8])))
        pos = hi * 64 + lo + quot
        addr[pl.ds(r, 1), :] = pos + lax.shift_right_logical(pos, 3) * 40
        return run + jnp.dot(hot_b, ones, preferred_element_type=f32)

    lax.fori_loop(0, n_rows, place_row, jnp.zeros((LANES, LANES), f32))

    for k in range(1, n_dev):
        src = lax.rem(me + n_dev - k, n_dev)
        pltpu.make_async_remote_copy(src_ref=hsend, dst_ref=hall.at[src], send_sem=ssem.at[k], recv_sem=rsem.at[k], device_id={'ep': src}, device_id_type=MESH).wait_recv()
    every = jnp.concatenate([hall[p, 0:1, :] for p in range(n_dev)], axis=0)
    loads, starts = slot_loads(every.astype(f32))
    meta[0:n_dev, :] = loads
    meta[n_dev:2 * n_dev, :] = starts
    slot_id = lane_u & (USTRIDE - 1)
    low = jnp.zeros((1, n_units), i32)
    high = jnp.zeros((1, n_units), i32)
    for s in range(n_slot):
        low = jnp.where(slot_id == s, lo_bound[s], low)
        high = jnp.where(slot_id == s, hi_bound[s], high)
    ends = loads + starts
    bad = jnp.where(valid & ((ends < low) | (ends > high)), 1.0, 0.0)
    flag[...] = jnp.broadcast_to(jnp.max(jnp.max(bad, axis=1, keepdims=True), axis=0, keepdims=True), flag.shape).astype(i32)
    for copy in sends:
        copy.wait_send()


def pack_kernel(addr, tok, send, wide, tmp):
    n_rows, n_col = addr.shape
    d_tiles = tok.shape[1] // LANES
    step = SUB * d_tiles

    @pl.loop(0, wide.shape[0] // step)
    def _(b):
        wide[pl.ds(pl.multiple_of(b * step, step), step), :] = jnp.zeros((step, LANES), jnp.float32)

    @pl.loop(0, n_rows)
    def _(r):
        @pl.loop(0, n_col // PACK)
        def _(c):
            row0 = pl.multiple_of(r * n_col + c * PACK, PACK)
            x = tok[pl.ds(row0, PACK), :].astype(jnp.float32)
            for h in range(PACK // SUB):
                for j in range(d_tiles):
                    tmp[h * step + j * SUB:h * step + (j + 1) * SUB, :] = x[h * SUB:(h + 1) * SUB, j * LANES:(j + 1) * LANES]
            for i in range(PACK):
                a = addr[r, c * PACK + i]
                wide[pl.ds(a, d_tiles, stride=SUB), :] = tmp[pl.ds((i // SUB) * step + i % SUB, d_tiles, stride=SUB), :]

    @pl.loop(0, send.shape[0] // PACK)
    def _(b):
        base = b * (2 * step)
        row0 = pl.multiple_of(b * PACK, PACK)
        for j in range(d_tiles):
            top = wide[pl.ds(base + j * SUB, SUB), :]
            bot = wide[pl.ds(base + step + j * SUB, SUB), :]
            send[pl.ds(row0, PACK), j * LANES:(j + 1) * LANES] = jnp.concatenate([top, bot], axis=0).astype(jnp.bfloat16)


def unpack_kernel(addr, gate, back, out, wide, tmp):
    n_rows, n_col = addr.shape
    d_tiles = out.shape[1] // LANES
    step = SUB * d_tiles

    @pl.loop(0, back.shape[0] // PACK)
    def _(b):
        base = b * (2 * step)
        row0 = pl.multiple_of(b * PACK, PACK)
        for j in range(d_tiles):
            x = back[pl.ds(row0, PACK), j * LANES:(j + 1) * LANES].astype(jnp.float32)
            wide[pl.ds(base + j * SUB, SUB), :] = x[:SUB]
            wide[pl.ds(base + step + j * SUB, SUB), :] = x[SUB:]

    @pl.loop(0, n_rows)
    def _(r):
        @pl.loop(0, n_col // PACK)
        def _(c):
            row0 = pl.multiple_of(r * n_col + c * PACK, PACK)
            for i in range(PACK):
                a = addr[r, c * PACK + i]
                g = gate[r, c * PACK + i]
                tmp[pl.ds((i // SUB) * step + i % SUB, d_tiles, stride=SUB), :] = wide[pl.ds(a, d_tiles, stride=SUB), :] * g
            for j in range(d_tiles):
                top = tmp[j * SUB:(j + 1) * SUB, :]
                bot = tmp[step + j * SUB:step + (j + 1) * SUB, :]
                out[pl.ds(row0, PACK), j * LANES:(j + 1) * LANES] = jnp.concatenate([top, bot], axis=0).astype(jnp.bfloat16)


def gelu(x):
    return x * (0.5 * (1.0 + jnp.tanh(0.7978845608028654 * (x + 0.044715 * (x * x * x)))))


def expert_kernel(cfg, meta, send, up_hbm, down_hbm, back, recv, xbuf, ybuf, up, down, hid, xs, win, dsend, drecv, rsend, rrecv, wsem):
    n_dev, n_slot, part = cfg['n_dev'], cfg['n_slot'], cfg['part']
    m_rows = n_dev * part
    d_model, d_ff = up_hbm.shape[1], up_hbm.shape[2]
    last, disp, ret, ret_lo = cfg['last'], cfg['disp'], cfg['ret'], cfg['ret_lo']
    n_grp = len(last)
    f32, bf16, i32 = jnp.float32, jnp.bfloat16, jnp.int32
    me = lax.axis_index('ep')

    def fetch(s, b):
        return (pltpu.make_async_copy(up_hbm.at[s], up.at[b], wsem.at[0, b]), pltpu.make_async_copy(down_hbm.at[s], down.at[b], wsem.at[1, b]))

    group_barrier(n_dev, me)

    def dispatch(j, k, peer):
        rows = pl.ds(disp[j], disp[j + 1] - disp[j])
        return pltpu.make_async_remote_copy(src_ref=send.at[k, rows], dst_ref=recv.at[k, rows], send_sem=dsend.at[j, k], recv_sem=drecv.at[j, k], device_id={'ep': peer}, device_id_type=MESH)

    def dispatch_own(j):
        rows = pl.ds(disp[j], disp[j + 1] - disp[j])
        return pltpu.make_async_copy(send.at[0, rows], recv.at[0, rows], drecv.at[j, 0])

    order = sorted(range(1, n_dev), key=lambda k: (abs(k - n_dev // 2), k))
    for j in range(n_grp):
        for k in order:
            dispatch(j, k, lax.rem(me + k, n_dev)).start()
        dispatch_own(j).start()
        if j == 0:
            for s in range(2):
                for copy in fetch(s, s):
                    copy.start()

    @pl.loop(0, n_dev)
    def _(k):
        @pl.loop(0, xbuf.shape[1])
        def _(b):
            xbuf[k, b] = jnp.zeros((PACK, d_model), bf16)

    def ffn(s, b):
        unit = me * USTRIDE + s
        lane = lax.broadcasted_iota(i32, (1, n_dev * WIN), 1)
        which = lax.shift_right_logical(lane, 6)
        off = jnp.zeros((1, n_dev * WIN), i32)
        num = jnp.zeros((1, n_dev * WIN), i32)
        for k in range(n_dev):
            src = lax.rem(me + n_dev - k, n_dev)
            load, start = meta[src, unit], meta[n_dev + src, unit]
            blk = lax.shift_right_logical(start, 4)
            base = blk * PACK
            for q in range(WIN // PACK):
                win[k * WIN + q * PACK:k * WIN + (q + 1) * PACK, :] = xbuf[k, blk + q]
            off = jnp.where(which == k, base - start, off)
            num = jnp.where(which == k, load, num)
        nth = (lane & (WIN - 1)) + off
        target = jnp.where((nth >= 0) & (nth < num), nth + which * part, -1)
        pick = (lax.broadcasted_iota(i32, (m_rows, n_dev * WIN), 0) == target).astype(bf16)
        xs[...] = jnp.dot(pick, win[...], preferred_element_type=f32).astype(bf16)
        tile = 512
        for t in range(d_ff // tile):
            pre = jnp.dot(xs[...], up[b, :, t * tile:(t + 1) * tile], preferred_element_type=f32)
            hid[:, t * tile:(t + 1) * tile] = gelu(pre).astype(bf16)
        tile = 256
        for t in range(d_model // tile):
            o = jnp.dot(hid[...], down[b, :, t * tile:(t + 1) * tile], preferred_element_type=f32).astype(bf16)
            for k in range(n_dev):
                ybuf[k, pl.ds(pl.multiple_of(s * part, PACK), part), t * tile:(t + 1) * tile] = o[k * part:(k + 1) * part]

    def give_back(j, k):
        rows = pl.ds(ret[j], ret[j + 1] - ret[j])
        peer = lax.rem(me + n_dev - k, n_dev)
        return pltpu.make_async_remote_copy(src_ref=recv.at[k, rows], dst_ref=back.at[k, rows], send_sem=rsend.at[j, k], recv_sem=rrecv.at[j, k], device_id={'ep': peer}, device_id_type=MESH)

    def give_own(j):
        rows = pl.ds(ret[j], ret[j + 1] - ret[j])
        return pltpu.make_async_copy(recv.at[0, rows], back.at[0, rows], rrecv.at[j, 0])

    def combine(j):
        n_rows = ret[j + 1] - ret[j]
        n_win = last[j] + 1 - ret_lo[j]
        width = n_win * part

        @pl.loop(0, n_dev)
        def _(i):
            k = lax.rem(n_dev // 2 + 3 * i, n_dev)
            src = lax.rem(me + n_dev - k, n_dev)
            lane = lax.broadcasted_iota(i32, (1, width), 1)
            target = jnp.full((1, width), -1, i32)
            for w in range(n_win):
                unit = me * USTRIDE + ret_lo[j] + w
                load, start = meta[src, unit], meta[n_dev + src, unit]
                nth = lane - w * part
                target = jnp.where((nth >= 0) & (nth < load), nth + start, target)
            pick = (lax.broadcasted_iota(i32, (n_rows, width), 0) + ret[j] == target).astype(bf16)
            rows = ybuf[k, ret_lo[j] * part:(last[j] + 1) * part, :]
            recv[k, ret[j]:ret[j + 1], :] = jnp.dot(pick, rows, preferred_element_type=f32).astype(bf16)

            @pl.when(k == 0)
            def _():
                give_own(j).start()

            @pl.when(k != 0)
            def _():
                give_back(j, k).start()

    @pl.loop(0, n_slot)
    def _(s):
        for j in range(n_grp):
            @pl.when(s == (0 if j == 0 else last[j - 1] + 1))
            def _():
                for k in range(1, n_dev):
                    dispatch(j, k, lax.rem(me + n_dev - k, n_dev)).wait_recv()
                dispatch_own(j).wait()

                @pl.loop(0, n_dev)
                def _(k):
                    @pl.loop(disp[j] // PACK, disp[j + 1] // PACK)
                    def _(b):
                        xbuf[k, b] = recv[k, pl.ds(pl.multiple_of(b * PACK, PACK), PACK), :]

        b = lax.rem(s, 2)
        for copy in fetch(s, b):
            copy.wait()
        ffn(s, b)

        @pl.when(s + 2 < n_slot)
        def _():
            for copy in fetch(s + 2, b):
                copy.start()

        for j in range(n_grp):
            @pl.when(s == last[j])
            def _():
                combine(j)

    for j in range(n_grp):
        for k in range(1, n_dev):
            dispatch(j, k, lax.rem(me + k, n_dev)).wait_send()
            give_back(j, k).wait_send()
            give_back(j, k).wait_recv()
        give_own(j).wait()


def plan(n_dev, n_slot, n_pairs, bound, z, lasts):
    stride = up_to(n_slot * bound, PACK)
    mean = n_pairs / (n_dev * n_slot)
    spread = 9.3 * mean / 30.1
    if z is None:
        hi = [bound * (s + 1) for s in range(n_slot)]
        lo = [0] * n_slot
    else:
        hi = [min(bound * (s + 1), math.ceil(mean * (s + 1) + z * spread * math.sqrt(s + 1))) for s in range(n_slot)]
        lo = [max(0, math.floor(mean * (s + 1) - z * spread * math.sqrt(s + 1))) for s in range(n_slot)]
        lo[-1] = 0
    cap = min(stride, up_to(hi[-1], PACK))
    hi[-1] = min(cap, n_slot * bound)
    disp = [0] + [up_to(hi[s], PACK) for s in lasts]
    disp[-1] = cap
    ret = [0] + [lo[s] // PACK * PACK for s in lasts]
    ret[-1] = cap
    ret_lo = [min(s for s in range(n_slot) if hi[s] > ret[j]) for j in range(len(lasts))]
    return dict(n_dev=n_dev, n_slot=n_slot, cap=cap, stride=stride, lo=lo, hi=hi, last=list(lasts), disp=disp, ret=ret, ret_lo=ret_lo, part=up_to(bound, PACK))


def solution(mesh):
    n_dev = mesh.shape['ep']

    def group_layer(tokens, topk_idx, topk_w, w_up, w_down, slot_expert):
        n_tok, d_model = tokens.shape
        n_slot = slot_expert.shape[1]
        d_ff = w_up.shape[3]
        n_pairs = n_tok * topk_idx.shape[1]
        base_load = n_pairs // (n_dev * n_slot)
        bound = base_load + base_load // 2 + 1
        fast = plan(n_dev, n_slot, n_pairs, bound, 3.33, [n_slot * 4 // 17 - 1, n_slot * 8 // 17 - 1, n_slot * 12 // 17 - 1, n_slot * 15 // 17 - 1, n_slot - 1])
        slow = plan(n_dev, n_slot, n_pairs, bound, None, [n_slot - 1])
        stride = fast['stride']
        n_rows = n_pairs // LANES
        n_units = n_dev * USTRIDE
        f32, bf16, i32 = jnp.float32, jnp.bfloat16, jnp.int32
        vmem = pl.BlockSpec(memory_space=pltpu.VMEM)
        smem = pl.BlockSpec(memory_space=pltpu.SMEM)
        hbm = pl.BlockSpec(memory_space=pl.ANY)
        big = 63 * 1024 * 1024

        addr, meta, flag = pl.pallas_call(
            functools.partial(route_kernel, n_dev, n_slot, stride, fast['lo'], fast['hi']),
            out_shape=[jax.ShapeDtypeStruct((n_rows, LANES), i32), jax.ShapeDtypeStruct((2 * n_dev, n_units), i32), jax.ShapeDtypeStruct((SUB, LANES), i32)],
            in_specs=[vmem, smem],
            out_specs=[vmem, vmem, vmem],
            scratch_shapes=[pltpu.VMEM((SUB, LANES), i32), pltpu.VMEM((n_dev, SUB, LANES), i32), pltpu.VMEM((n_units, LANES), i32), pltpu.SemaphoreType.DMA((n_dev,)), pltpu.SemaphoreType.DMA((n_dev,))],
            compiler_params=pltpu.CompilerParams(collective_id=0, has_side_effects=True),
            name='route',
        )(topk_idx.reshape(n_rows, LANES), slot_expert)

        d_tiles = d_model // LANES
        wide = pltpu.VMEM((n_dev * stride * d_tiles, LANES), f32)
        tmp = pltpu.VMEM((PACK * d_tiles, LANES), f32)
        send = pl.pallas_call(
            pack_kernel,
            out_shape=jax.ShapeDtypeStruct((n_dev * stride, d_model), bf16),
            in_specs=[smem, vmem],
            out_specs=vmem,
            scratch_shapes=[wide, tmp],
            compiler_params=pltpu.CompilerParams(vmem_limit_bytes=big),
            name='pack',
        )(addr, tokens).reshape(n_dev, stride, d_model)

        def run(cfg, meta, send, w_up, w_down):
            n_grp = len(cfg['last'])
            part, cap = cfg['part'], cfg['cap']
            m_rows = n_dev * part
            dma = pltpu.SemaphoreType.DMA((n_grp, n_dev))
            return pl.pallas_call(
                functools.partial(expert_kernel, cfg),
                out_shape=jax.ShapeDtypeStruct((n_dev, stride, d_model), bf16),
                in_specs=[smem, hbm, hbm, hbm],
                out_specs=hbm,
                scratch_shapes=[
                    pltpu.VMEM((n_dev, cap, d_model), bf16),
                    pltpu.VMEM((n_dev, (cap + WIN) // PACK, PACK, d_model), bf16),
                    pltpu.VMEM((n_dev, n_slot * part, d_model), bf16),
                    pltpu.VMEM((2, d_model, d_ff), bf16),
                    pltpu.VMEM((2, d_ff, d_model), bf16),
                    pltpu.VMEM((m_rows, d_ff), bf16),
                    pltpu.VMEM((m_rows, d_model), bf16),
                    pltpu.VMEM((n_dev * WIN, d_model), bf16),
                    dma, dma, dma, dma,
                    pltpu.SemaphoreType.DMA((2, 2)),
                ],
                compiler_params=pltpu.CompilerParams(collective_id=1, has_side_effects=True, vmem_limit_bytes=big),
                name='experts',
            )(meta, send, w_up, w_down)

        back = lax.cond(flag[0, 0] == 0, functools.partial(run, fast), functools.partial(run, slow), meta, send, w_up[0], w_down[0])

        return pl.pallas_call(
            unpack_kernel,
            out_shape=jax.ShapeDtypeStruct((n_tok, d_model), bf16),
            in_specs=[smem, smem, vmem],
            out_specs=vmem,
            scratch_shapes=[wide, tmp],
            compiler_params=pltpu.CompilerParams(vmem_limit_bytes=big),
            name='unpack',
        )(addr, topk_w.reshape(n_rows, LANES), back.reshape(n_dev * stride, d_model))

    row_spec = P(('dp', 'ep'), None)
    weight_spec = P('ep', None, None, None)
    return jax.shard_map(group_layer, mesh=mesh, in_specs=(row_spec, row_spec, row_spec, weight_spec, weight_spec, P(None, None)), out_specs=row_spec, check_vma=False)
```

time: 544 us -> 238 us (0.44)
  Pallas kernels: 0 us -> 236 us
  local copies, waits for them, and re-layouts: 189 us -> 1.19 us
  blocking collectives: 118 us -> 0 us
  waiting for transfers between devices: 111 us -> 0 us
  matrix products: 103 us -> 0 us
  other arithmetic: 14.9 us -> 0 us
  starting transfers between devices: 5.76 us -> 0 us
    pallas_call x0 -> x4, Pallas kernels: none -> 236 us  [the longest x1 175 us: run(): pl.pallas_call(functools.partial(expert_kernel, cfg), out_shape=jax.Shape...]
    all_to_all x1 -> x0, blocking collectives: 118 us -> none  [group_layer(): recv_buf = lax.all_to_all(send_buf, 'ep', 1, 1, tiled=True)]
    all_to_all x1 -> x0, waiting for transfers between devices: 111 us -> none  [group_layer(): back_buf = lax.all_to_all(expert_out, 'ep', 1, 1, tiled=True)]
    gather x4 -> x0, local copies, waits for them, and re-layouts: 109 us -> none  [the longest x1 33.1 us: route_pairs(): slot_flat = slot_of[flat_exp, pair_rank % pair_copies]]
    dot_general x2 -> x0, matrix products: 103 us -> none  [the longest x1 54.2 us: expert_ffn(): jnp.einsum('spcm,smf->spcf', recv_buf, up_local, preferred_element_type=j...]
    reshape x4 -> x0, local copies, waits for them, and re-layouts: 37 us -> none  [the longest x2 22.2 us: group_layer(): send_buf = tokens[buf_tok].reshape(n_slot, n_dev, capacity, d_model)]
    scatter x2 -> x0, local copies, waits for them, and re-layouts: 22.8 us -> none  [the longest x1 15.7 us: route_pairs(): jnp.zeros((n_slot * n_dev * capacity,), jnp.int32).at[pair_pos]]
    all_to_all x1 -> x0, local copies, waits for them, and re-layouts: 8.77 us -> none  [group_layer(): back_buf = lax.all_to_all(expert_out, 'ep', 1, 1, tiled=True)]
  transfers between devices with their start and end apart: 1 -> 0, of which waited for: 1 -> 0; matrix products, arithmetic and copies ran while one was open for 0% -> 0% of each run, Pallas kernels for 0% -> 0%
where the time goes in v1:
time: 238 us
  Pallas kernels  236 us (99%)
    pallas_call x1, Pallas kernels, run(): pl.pallas_call(functools.partial(expert_kernel, cfg), out_shape=jax.Shape...  175 us
    pallas_call x1, Pallas kernels, group_layer(): pl.pallas_call(pack_kernel, out_shape=jax.ShapeDtypeStruct((n_dev * strid...  24.4 us
    pallas_call x1, Pallas kernels, group_layer(): pl.pallas_call(unpack_kernel, out_shape=jax.ShapeDtypeStruct((n_tok, d_mo...  23.6 us
    pallas_call x1, Pallas kernels, group_layer(): pl.pallas_call(functools.partial(route_kernel, n_dev, n_slot, stride, fas...  13.3 us

profile of v1, /device:TPU:113, one launch (start us, length us, event | category | flops | bytes accessed | tf_op | source)
XLA Modules:
  0.0 237.9 jit_solution(8840812995831045084)
XLA Ops:
  0.0 13.3 %route.1 = (s32[32,128]{1,0:T(8,128)}, s32[16,256]{1,0:T(8,128)S(1)}, s32[8,128]{1,0:T(8,128)}) custom-call(s32[32,128]{1,0:T(8,128)} %bitcast.15, s32[8,17]{1,0:T(8,128)} %table.1), custom_call_target="tpu_custom_call" | custom-call | tf_op jit(solution)/shard_map/route/pallas_call | solution.py:379
  13.3 1.2 slice.3
  15.1 24.4 %pack.1 = bf16[6272,768]{1,0:T(8,128)(2,1)} custom-call(s32[32,128]{1,0:T(8,128)} %get-tuple-element.42.addr, bf16[4096,768]{1,0:T(8,128)(2,1)} %tok.1), custom_call_target="tpu_custom_call" | custom-call | tf_op jit(solution)/shard_map/pack/pallas_call | solution.py:392
  39.5 174.8 %conditional.1 = (bf16[6272,768]{1,0:T(8,128)(2,1)}) conditional(s32[]{:T(128)} %bitcast.10, (bf16[6272,768]{1,0:T(8,128)(2,1)}, bf16[1,17,768,3072]{3,2,1,0:T(8,128)(2,1)}, bf16[1,17,3072,768]{3,2,1,0:T(8,128)(2,1)}, s32[16,256]{1,0:T(8,128)S(1)}) %tuple.13, (bf16[6272,768]{1,0:T(8,128)(2,1)}, bf16[1,17,768,3072]{3,2,1,0:T(8,128)(2,1)}, ...), branch_computations={%region_0.0_spmd, %region_1.0_spmd} | conditional | bytes 8 | solution.py:428
  39.5 174.8 %experts.3 = bf16[8,784,768]{2,1,0:T(8,128)(2,1)} custom-call(s32[16,256]{1,0:T(8,128)S(1)} %get-tuple-element.35.meta, bf16[8,784,768]{2,1,0:T(8,128)(2,1)} %bitcast.12, bf16[17,768,3072]{2,1,0:T(8,128)(2,1)} %bitcast.5.up_hbm, bf16[17,3072,768]{2,1,0:T(8,128)(2,1)} %bitcast.6.down_hbm), custom_call_target="tpu_custom_call" | custom-call | tf_op jit(solution)/shard_map/cond/branch_1_fun/experts/pallas_call | solution.py:407
  214.3 23.6 %unpack.1 = bf16[4096,768]{1,0:T(8,128)(2,1)} custom-call(s32[32,128]{1,0:T(8,128)} %get-tuple-element.42.addr, f32[32,128]{1,0:T(8,128)} %bitcast.16, bf16[6272,768]{1,0:T(8,128)(2,1)} %get-tuple-element.45.back), custom_call_target="tpu_custom_call" | custom-call | tf_op jit(solution)/shard_map/unpack/pallas_call | solution.py:430

commit v2 on v1

--- a/solution.py
+++ b/solution.py
@@ -127,65 +127,132 @@
         copy.wait_send()
 
 
-def pack_kernel(addr, tok, send, wide, tmp):
+def pack_kernel(cap, addr, flag, tok_hbm, send, tok, wide, tmp, stage, tsem, ssem):
     n_rows, n_col = addr.shape
+    n_dev, stride = stage.shape[0], stage.shape[1]
     d_tiles = tok.shape[1] // LANES
     step = SUB * d_tiles
-
-    @pl.loop(0, wide.shape[0] // step)
+    load = pltpu.make_async_copy(tok_hbm, tok, tsem)
+    load.start()
+    zero_rows = 4 * step
+
+    @pl.loop(0, wide.shape[0] // zero_rows)
     def _(b):
-        wide[pl.ds(pl.multiple_of(b * step, step), step), :] = jnp.zeros((step, LANES), jnp.float32)
+        wide[pl.ds(pl.multiple_of(b * zero_rows, zero_rows), zero_rows), :] = jnp.zeros((zero_rows, LANES), jnp.float32)
+
+    load.wait()
 
     @pl.loop(0, n_rows)
     def _(r):
-        @pl.loop(0, n_col // PACK)
-        def _(c):
-            row0 = pl.multiple_of(r * n_col + c * PACK, PACK)
-            x = tok[pl.ds(row0, PACK), :].astype(jnp.float32)
+        for c in range(n_col // PACK):
+            at = c * 2 * step
+            x = tok[pl.ds(pl.multiple_of(r * n_col + c * PACK, PACK), PACK), :].astype(jnp.float32)
             for h in range(PACK // SUB):
                 for j in range(d_tiles):
-                    tmp[h * step + j * SUB:h * step + (j + 1) * SUB, :] = x[h * SUB:(h + 1) * SUB, j * LANES:(j + 1) * LANES]
+                    tmp[at + h * step + j * SUB:at + h * step + (j + 1) * SUB, :] = x[h * SUB:(h + 1) * SUB, j * LANES:(j + 1) * LANES]
             for i in range(PACK):
                 a = addr[r, c * PACK + i]
-                wide[pl.ds(a, d_tiles, stride=SUB), :] = tmp[pl.ds((i // SUB) * step + i % SUB, d_tiles, stride=SUB), :]
-
-    @pl.loop(0, send.shape[0] // PACK)
-    def _(b):
-        base = b * (2 * step)
-        row0 = pl.multiple_of(b * PACK, PACK)
+                wide[pl.ds(a, d_tiles, stride=SUB), :] = tmp[pl.ds(at + (i // SUB) * step + i % SUB, d_tiles, stride=SUB), :]
+
+    def narrow(k, b):
+        base = (k * (stride // PACK) + b) * (2 * step)
+        rows = pl.ds(pl.multiple_of(b * PACK, PACK), PACK)
         for j in range(d_tiles):
             top = wide[pl.ds(base + j * SUB, SUB), :]
             bot = wide[pl.ds(base + step + j * SUB, SUB), :]
-            send[pl.ds(row0, PACK), j * LANES:(j + 1) * LANES] = jnp.concatenate([top, bot], axis=0).astype(jnp.bfloat16)
-
-
-def unpack_kernel(addr, gate, back, out, wide, tmp):
+            stage[k, rows, j * LANES:(j + 1) * LANES] = jnp.concatenate([top, bot], axis=0).astype(jnp.bfloat16)
+
+    def store(k, lo, hi):
+        return pltpu.make_async_copy(stage.at[k, pl.ds(lo, hi - lo)], send.at[k, pl.ds(lo, hi - lo)], ssem.at[k])
+
+    @pl.loop(0, n_dev)
+    def _(k):
+        @pl.loop(0, cap // PACK, unroll=4)
+        def _(b):
+            narrow(k, b)
+
+        store(k, 0, cap).start()
+
+    @pl.loop(0, n_dev)
+    def _(k):
+        store(k, 0, cap).wait()
+
+    @pl.when(flag[0, 0] != 0)
+    def _():
+        @pl.loop(0, n_dev)
+        def _(k):
+            @pl.loop(cap // PACK, stride // PACK)
+            def _(b):
+                narrow(k, b)
+
+            rest = store(k, cap, stride)
+            rest.start()
+            rest.wait()
+
+
+def unpack_kernel(cap, addr, flag, gate, back_hbm, out_hbm, back, wide, tmp, out, bsem, osem):
     n_rows, n_col = addr.shape
+    n_dev, stride = back.shape[0], back.shape[1]
     d_tiles = out.shape[1] // LANES
     step = SUB * d_tiles
 
-    @pl.loop(0, back.shape[0] // PACK)
-    def _(b):
-        base = b * (2 * step)
-        row0 = pl.multiple_of(b * PACK, PACK)
+    def load(k, lo, hi):
+        return pltpu.make_async_copy(back_hbm.at[k, pl.ds(lo, hi - lo)], back.at[k, pl.ds(lo, hi - lo)], bsem.at[k])
+
+    def widen(k, b):
+        base = (k * (stride // PACK) + b) * (2 * step)
+        rows = pl.ds(pl.multiple_of(b * PACK, PACK), PACK)
         for j in range(d_tiles):
-            x = back[pl.ds(row0, PACK), j * LANES:(j + 1) * LANES].astype(jnp.float32)
+            x = back[k, rows, j * LANES:(j + 1) * LANES].astype(jnp.float32)
             wide[pl.ds(base + j * SUB, SUB), :] = x[:SUB]
             wide[pl.ds(base + step + j * SUB, SUB), :] = x[SUB:]
 
+    @pl.loop(0, n_dev)
+    def _(k):
+        load(k, 0, cap).start()
+
+    @pl.loop(0, n_dev)
+    def _(k):
+        load(k, 0, cap).wait()
+
+        @pl.loop(0, cap // PACK, unroll=4)
+        def _(b):
+            widen(k, b)
+
+    @pl.when(flag[0, 0] != 0)
+    def _():
+        @pl.loop(0, n_dev)
+        def _(k):
+            rest = load(k, cap, stride)
+            rest.start()
+            rest.wait()
+
+            @pl.loop(cap // PACK, stride // PACK)
+            def _(b):
+                widen(k, b)
+
+    def give(g):
+        rows = pl.ds(pl.multiple_of(g * n_col, n_col), n_col)
+        return pltpu.make_async_copy(out.at[rows], out_hbm.at[rows], osem)
+
     @pl.loop(0, n_rows)
     def _(r):
-        @pl.loop(0, n_col // PACK)
-        def _(c):
-            row0 = pl.multiple_of(r * n_col + c * PACK, PACK)
+        for c in range(n_col // PACK):
+            at = c * 2 * step
             for i in range(PACK):
                 a = addr[r, c * PACK + i]
                 g = gate[r, c * PACK + i]
-                tmp[pl.ds((i // SUB) * step + i % SUB, d_tiles, stride=SUB), :] = wide[pl.ds(a, d_tiles, stride=SUB), :] * g
+                tmp[pl.ds(at + (i // SUB) * step + i % SUB, d_tiles, stride=SUB), :] = wide[pl.ds(a, d_tiles, stride=SUB), :] * g
+            rows = pl.ds(pl.multiple_of(r * n_col + c * PACK, PACK), PACK)
             for j in range(d_tiles):
-                top = tmp[j * SUB:(j + 1) * SUB, :]
-                bot = tmp[step + j * SUB:step + (j + 1) * SUB, :]
-                out[pl.ds(row0, PACK), j * LANES:(j + 1) * LANES] = jnp.concatenate([top, bot], axis=0).astype(jnp.bfloat16)
+                top = tmp[at + j * SUB:at + (j + 1) * SUB, :]
+                bot = tmp[at + step + j * SUB:at + step + (j + 1) * SUB, :]
+                out[rows, j * LANES:(j + 1) * LANES] = jnp.concatenate([top, bot], axis=0).astype(jnp.bfloat16)
+        give(r).start()
+
+    @pl.loop(0, n_rows)
+    def _(r):
+        give(r).wait()
 
 
 def gelu(x):
@@ -334,7 +401,7 @@
         give_own(j).wait()
 
 
-def plan(n_dev, n_slot, n_pairs, bound, z, lasts):
+def plan(n_dev, n_slot, n_pairs, bound, z, z_cap, lasts):
     stride = up_to(n_slot * bound, PACK)
     mean = n_pairs / (n_dev * n_slot)
     spread = 9.3 * mean / 30.1
@@ -345,10 +412,10 @@
         hi = [min(bound * (s + 1), math.ceil(mean * (s + 1) + z * spread * math.sqrt(s + 1))) for s in range(n_slot)]
         lo = [max(0, math.floor(mean * (s + 1) - z * spread * math.sqrt(s + 1))) for s in range(n_slot)]
         lo[-1] = 0
-    cap = min(stride, up_to(hi[-1], PACK))
-    hi[-1] = min(cap, n_slot * bound)
+    cap = stride if z is None else min(stride, up_to(math.ceil(mean * n_slot + z_cap * spread * math.sqrt(n_slot)), PACK))
+    hi = [min(h, cap) for h in hi]
     disp = [0] + [up_to(hi[s], PACK) for s in lasts]
-    disp[-1] = cap
+    disp = [min(d, cap) for d in disp[:-1]] + [cap]
     ret = [0] + [lo[s] // PACK * PACK for s in lasts]
     ret[-1] = cap
     ret_lo = [min(s for s in range(n_slot) if hi[s] > ret[j]) for j in range(len(lasts))]
@@ -365,8 +432,8 @@
         n_pairs = n_tok * topk_idx.shape[1]
         base_load = n_pairs // (n_dev * n_slot)
         bound = base_load + base_load // 2 + 1
-        fast = plan(n_dev, n_slot, n_pairs, bound, 3.33, [n_slot * 4 // 17 - 1, n_slot * 8 // 17 - 1, n_slot * 12 // 17 - 1, n_slot * 15 // 17 - 1, n_slot - 1])
-        slow = plan(n_dev, n_slot, n_pairs, bound, None, [n_slot - 1])
+        fast = plan(n_dev, n_slot, n_pairs, bound, 3.6, 2.9, [n_slot * 4 // 17 - 1, n_slot * 8 // 17 - 1, n_slot * 12 // 17 - 1, n_slot * 15 // 17 - 1, n_slot - 1])
+        slow = plan(n_dev, n_slot, n_pairs, bound, None, None, [n_slot - 1])
         stride = fast['stride']
         n_rows = n_pairs // LANES
         n_units = n_dev * USTRIDE
@@ -388,16 +455,19 @@
 
         d_tiles = d_model // LANES
         wide = pltpu.VMEM((n_dev * stride * d_tiles, LANES), f32)
-        tmp = pltpu.VMEM((PACK * d_tiles, LANES), f32)
+        tmp = pltpu.VMEM((LANES * d_tiles, LANES), f32)
+        block = pltpu.VMEM((n_dev, stride, d_model), bf16)
+        rows_vmem = pltpu.VMEM((n_tok, d_model), bf16)
+        sem, sems = pltpu.SemaphoreType.DMA, pltpu.SemaphoreType.DMA((n_dev,))
         send = pl.pallas_call(
-            pack_kernel,
-            out_shape=jax.ShapeDtypeStruct((n_dev * stride, d_model), bf16),
-            in_specs=[smem, vmem],
-            out_specs=vmem,
-            scratch_shapes=[wide, tmp],
+            functools.partial(pack_kernel, fast['cap']),
+            out_shape=jax.ShapeDtypeStruct((n_dev, stride, d_model), bf16),
+            in_specs=[smem, smem, hbm],
+            out_specs=hbm,
+            scratch_shapes=[rows_vmem, wide, tmp, block, sem, sems],
             compiler_params=pltpu.CompilerParams(vmem_limit_bytes=big),
             name='pack',
-        )(addr, tokens).reshape(n_dev, stride, d_model)
+        )(addr, flag, tokens)
 
         def run(cfg, meta, send, w_up, w_down):
             n_grp = len(cfg['last'])
@@ -428,14 +498,14 @@
         back = lax.cond(flag[0, 0] == 0, functools.partial(run, fast), functools.partial(run, slow), meta, send, w_up[0], w_down[0])
 
         return pl.pallas_call(
-            unpack_kernel,
+            functools.partial(unpack_kernel, fast['cap']),
             out_shape=jax.ShapeDtypeStruct((n_tok, d_model), bf16),
-            in_specs=[smem, smem, vmem],
-            out_specs=vmem,
-            scratch_shapes=[wide, tmp],
+            in_specs=[smem, smem, smem, hbm],
+            out_specs=hbm,
+            scratch_shapes=[block, wide, tmp, rows_vmem, sems, sem],
             compiler_params=pltpu.CompilerParams(vmem_limit_bytes=big),
             name='unpack',
-        )(addr, topk_w.reshape(n_rows, LANES), back.reshape(n_dev * stride, d_model))
+        )(addr, flag, topk_w.reshape(n_rows, LANES), back)
 
     row_spec = P(('dp', 'ep'), None)
     weight_spec = P('ep', None, None, None)

time: 238 us -> 214 us (0.90)
  Pallas kernels: 236 us -> 211 us
    pallas_call x2, Pallas kernels: 47.9 us -> 27.1 us  [the longest x1 13.8 us: group_layer(): pl.pallas_call(functools.partial(unpack_kernel, fast['cap']), out_shape=j...]
    pallas_call x1, Pallas kernels: 175 us -> 171 us  [run(): pl.pallas_call(functools.partial(expert_kernel, cfg), out_shape=jax.Shape...]
where the time goes in v2:
time: 214 us; the launch traced here: 213 us
  Pallas kernels  211 us (99%)
    pallas_call x1, Pallas kernels, run(): pl.pallas_call(functools.partial(expert_kernel, cfg), out_shape=jax.Shape...  171 us
    pallas_call x1, Pallas kernels, group_layer(): pl.pallas_call(functools.partial(unpack_kernel, fast['cap']), out_shape=j...  13.8 us
    pallas_call x1, Pallas kernels, group_layer(): pl.pallas_call(functools.partial(route_kernel, n_dev, n_slot, stride, fas...  13.3 us
    pallas_call x1, Pallas kernels, group_layer(): pl.pallas_call(functools.partial(pack_kernel, fast['cap']), out_shape=jax...  13.2 us

profile of v2, /device:TPU:113, one launch (start us, length us, event | category | flops | bytes accessed | tf_op | source)
XLA Modules:
  0.0 213.2 jit_solution(6984360118066596230)
XLA Ops:
  0.0 13.3 %route.1 = (s32[32,128]{1,0:T(8,128)}, s32[16,256]{1,0:T(8,128)S(1)}, s32[8,128]{1,0:T(8,128)}) custom-call(s32[32,128]{1,0:T(8,128)} %bitcast.6, s32[8,17]{1,0:T(8,128)} %table.1), custom_call_target="tpu_custom_call" | custom-call | tf_op jit(solution)/shard_map/route/pallas_call | solution.py:446
  13.3 1.2 slice.3
  15.1 13.2 %pack.1 = bf16[8,784,768]{2,1,0:T(8,128)(2,1)} custom-call(s32[32,128]{1,0:T(8,128)} %get-tuple-element.35.addr, s32[8,128]{1,0:T(8,128)} %get-tuple-element.36.flag, bf16[4096,768]{1,0:T(8,128)(2,1)} %tok_hbm.1), custom_call_target="tpu_custom_call" | custom-call | tf_op jit(solution)/shard_map/pack/pallas_call | solution.py:462
  28.4 170.8 %conditional.1 = (bf16[8,784,768]{2,1,0:T(8,128)(2,1)}) conditional(s32[]{:T(128)} %bitcast.2, (s32[16,256]{1,0:T(8,128)S(1)}, bf16[8,784,768]{2,1,0:T(8,128)(2,1)}, bf16[17,768,3072]{2,1,0:T(8,128)(2,1)}, bf16[17,3072,768]{2,1,0:T(8,128)(2,1)}) %tuple.11, (s32[16,256]{1,0:T(8,128)S(1)}, bf16[8,784,768]{2,1,0:T(8,128)(2,1)}, ...), branch_computations={%region_0.0_spmd, %region_1.0_spmd} | conditional | bytes 8 | solution.py:498
  28.6 170.6 %experts.3 = bf16[8,784,768]{2,1,0:T(8,128)(2,1)} custom-call(s32[16,256]{1,0:T(8,128)S(1)} %get-tuple-element.28.meta, bf16[8,784,768]{2,1,0:T(8,128)(2,1)} %get-tuple-element.29.send, bf16[17,768,3072]{2,1,0:T(8,128)(2,1)} %get-tuple-element.30.up_hbm, bf16[17,3072,768]{2,1,0:T(8,128)(2,1)} %get-tuple-element.31.down_hbm), custom_call_target="tpu_custom_call" | custom-call | tf_op jit(solution)/shard_map/cond/branch_1_fun/experts/pallas_call | solution.py:477
  199.2 13.8 %unpack.1 = bf16[4096,768]{1,0:T(8,128)(2,1)} custom-call(s32[32,128]{1,0:T(8,128)} %get-tuple-element.35.addr, s32[8,128]{1,0:T(8,128)} %get-tuple-element.36.flag, f32[32,128]{1,0:T(8,128)} %bitcast.5, bf16[8,784,768]{2,1,0:T(8,128)(2,1)} %get-tuple-element.38.back_hbm), custom_call_target="tpu_custom_call" | custom-call | tf_op jit(solution)/shard_map/unpack/pallas_call | solution.py:500

commit v3 on v2

--- a/solution.py
+++ b/solution.py
@@ -14,13 +14,7 @@
 PACK = 16
 USTRIDE = 32
 WIN = 64
-
-
-def div_small(x, c):
-    third = lax.shift_right_logical(x * 171, 9)
-    quarter = lax.shift_right_logical(x, 2)
-    half = lax.shift_right_logical(x, 1)
-    return jnp.where(c == 1, x, jnp.where(c == 2, half, jnp.where(c == 3, third, quarter)))
+TIERS = (1.125, 1.156, 1.1875, 1.25)
 
 
 def up_to(x, m):
@@ -34,27 +28,76 @@
     pl.semaphore_wait(barrier, n_dev - 1)
 
 
-def route_kernel(n_dev, n_slot, stride, lo_bound, hi_bound, idx, table, addr, meta, flag, hsend, hall, tabcol, ssem, rsem):
+def level_copies(loads, where, copies, bound):
+    n_copy = len(where)
+    f32, bf16 = jnp.float32, jnp.bfloat16
+    share = [jnp.where(k < copies, loads / jnp.maximum(copies, 1.0), 0.0) for k in range(n_copy)]
+    for _ in range(2):
+        block = sum(lax.dot_general(share[k].astype(bf16), where[k], (((1,), (1,)), ((), ())), preferred_element_type=f32) for k in range(n_copy))
+        there = [jnp.where(k < copies, jnp.dot(block.astype(bf16), where[k], preferred_element_type=f32), 0.0) for k in range(n_copy)]
+        mean = sum(there) / jnp.maximum(copies, 1.0)
+        share = [jnp.where(k < copies, jnp.clip(share[k] + 0.5 * (mean - there[k]), 0.0, bound), 0.0) for k in range(n_copy)]
+    left, taken = loads, []
+    for k in range(n_copy):
+        after = jnp.maximum(copies - (k + 1), 0.0)
+        want = jnp.floor(share[k] + 0.5)
+        got = jnp.minimum(jnp.maximum(want, jnp.maximum(left - bound * after, 0.0)), jnp.minimum(left, bound))
+        got = jnp.where(k < copies, got, 0.0)
+        taken.append(got)
+        left = left - got
+    return taken
+
+
+def route_kernel(n_dev, n_slot, stride, bound, low, high, caps, idx, table, addr, meta, flag, hsend, hall, hrow, tabcol, cums, ssem, rsem):
     me = lax.axis_index('ep')
     f32, bf16, i32 = jnp.float32, jnp.bfloat16, jnp.int32
     n_rows = idx.shape[0]
     n_units = n_dev * USTRIDE
+    n_copy = 4
+    nt = (((1,), (1,)), ((), ()))
     group_barrier(n_dev, me)
     sub_e = lax.broadcasted_iota(i32, (LANES, LANES), 0)
     lane_e = lax.broadcasted_iota(i32, (LANES, LANES), 1)
-
-    def count_row(r, acc):
-        return acc + (sub_e == idx[pl.ds(r, 1), :]).astype(f32)
-
-    seen = lax.fori_loop(0, n_rows, count_row, jnp.zeros((LANES, LANES), f32))
-    hist = lax.dot_general(jnp.ones((SUB, LANES), bf16), seen.astype(bf16), (((1,), (1,)), ((), ())), preferred_element_type=f32)
-    hsend[...] = hist.astype(i32)
-    hall[me] = hist.astype(i32)
+    ones = jnp.ones((SUB, LANES), bf16)
+
+    @pl.loop(0, n_rows // SUB)
+    def _(g):
+        base = pl.multiple_of(g * SUB, SUB)
+        rows = idx[pl.ds(base, SUB), :]
+        parts = []
+        for r in range(SUB):
+            hot = (sub_e == rows[r:r + 1, :]).astype(bf16)
+            parts.append(lax.dot_general(ones, hot, nt, preferred_element_type=f32)[0:1])
+        hrow[pl.ds(base, SUB), :] = jnp.concatenate(parts, axis=0)
+
+    hrows = hrow[...]
+    hist = jnp.broadcast_to(jnp.sum(hrows, axis=0, keepdims=True), (SUB, LANES)).astype(i32)
+    hsend[...] = hist
+    hall[me] = hist
     sends = []
     for k in range(1, n_dev):
         copy = pltpu.make_async_remote_copy(src_ref=hsend, dst_ref=hall.at[me], send_sem=ssem.at[k], recv_sem=rsem.at[k], device_id={'ep': lax.rem(me + k, n_dev)}, device_id_type=MESH)
         copy.start()
         sends.append(copy)
+
+    rr = lax.broadcasted_iota(i32, (n_rows, n_rows), 0)
+    cc = lax.broadcasted_iota(i32, (n_rows, n_rows), 1)
+    hrow[...] = jnp.dot((cc < rr).astype(bf16), hrows.astype(bf16), preferred_element_type=f32)
+    tri = (sub_e < lane_e).astype(bf16)
+
+    @pl.loop(0, n_rows // SUB)
+    def _(g):
+        base = pl.multiple_of(g * SUB, SUB)
+        rows = idx[pl.ds(base, SUB), :]
+        runs = hrow[pl.ds(base, SUB), :].astype(bf16)
+        parts = []
+        for r in range(SUB):
+            hot = sub_e == rows[r:r + 1, :]
+            hot_b = hot.astype(bf16)
+            prefix = jnp.dot(hot_b, tri, preferred_element_type=f32)
+            run = jnp.dot(runs, hot_b, preferred_element_type=f32)[r:r + 1]
+            parts.append(jnp.sum(jnp.where(hot, prefix, 0.0), axis=0, keepdims=True) + run)
+        addr[pl.ds(base, SUB), :] = jnp.concatenate(parts, axis=0).astype(i32)
 
     lane_u = lax.broadcasted_iota(i32, (1, n_units), 1)
     tabrow = jnp.full((1, n_units), -1, i32)
@@ -69,65 +112,75 @@
     same = jnp.concatenate([tcol] * (n_units // LANES), axis=1) == tabrow
     su = lax.broadcasted_iota(i32, (n_units, n_units), 0)
     lu = lax.broadcasted_iota(i32, (n_units, n_units), 1)
-    copy_rank = jnp.sum(jnp.where(same & (su < lu), 1.0, 0.0), axis=0, keepdims=True).astype(i32)
-    copies = jnp.sum(jnp.where(same, 1.0, 0.0), axis=0, keepdims=True).astype(i32)
     valid = tabrow >= 0
+    copy_rank = jnp.where(valid, jnp.sum(jnp.where(same & (su < lu), 1.0, 0.0), axis=0, keepdims=True).astype(i32), -1)
     before = ((su < lu) & (lax.shift_right_logical(su, 5) == lax.shift_right_logical(lu, 5))).astype(bf16)
-
-    def slot_loads(h):
-        per_unit = lax.dot_general(h.astype(bf16), unit_exp, (((1,), (1,)), ((), ())), preferred_element_type=f32).astype(i32)
-        loads = jnp.where(valid, div_small(per_unit - copy_rank + copies - 1, copies), 0)
-        starts = jnp.dot(loads.astype(bf16), before, preferred_element_type=f32).astype(i32)
-        return loads, starts
-
-    _, own_starts = slot_loads(hist)
-    block = lax.rem(lax.shift_right_logical(lane_u, 5) + n_dev - me, n_dev)
-    first = jnp.concatenate([own_starts, own_starts], axis=0) + block * stride
-    row16 = lax.broadcasted_iota(i32, (2 * SUB, n_units), 0)
-    part = jnp.where(row16 < 4, lax.shift_right_logical(first, 6), jnp.where(row16 < 8, first & 63, copies))
-    chosen = (copy_rank == (row16 & 3)) & valid & (row16 < 9)
-    exp_tab = jnp.dot(jnp.where(chosen, part, 0).astype(bf16), unit_exp, preferred_element_type=f32).astype(bf16)
-    tri = (sub_e < lane_e).astype(bf16)
-    ones = jnp.ones((LANES, LANES), bf16)
-
-    def place_row(r, run):
-        hot = sub_e == idx[pl.ds(r, 1), :]
-        hot_b = hot.astype(bf16)
-        prefix = jnp.dot(hot_b, tri, preferred_element_type=f32) + run
-        rank = jnp.sum(jnp.where(hot, prefix, 0.0), axis=0, keepdims=True).astype(i32)
-        got = jnp.dot(exp_tab, hot_b, preferred_element_type=f32).astype(i32)
-        c = got[8:9]
-        quot = div_small(rank, c)
-        kk = rank - quot * c
-        hi = jnp.where(kk == 0, got[0:1], jnp.where(kk == 1, got[1:2], jnp.where(kk == 2, got[2:3], got[3:4])))
-        lo = jnp.where(kk == 0, got[4:5], jnp.where(kk == 1, got[5:6], jnp.where(kk == 2, got[6:7], got[7:8])))
-        pos = hi * 64 + lo + quot
-        addr[pl.ds(r, 1), :] = pos + lax.shift_right_logical(pos, 3) * 40
-        return run + jnp.dot(hot_b, ones, preferred_element_type=f32)
-
-    lax.fori_loop(0, n_rows, place_row, jnp.zeros((LANES, LANES), f32))
+    copies = jnp.dot(jnp.ones((SUB, n_units), bf16), unit_exp, preferred_element_type=f32)[0:1]
+    dev8 = lax.broadcasted_iota(i32, (SUB, n_units), 0)
+    dev_u = lax.shift_right_logical(lane_u, 5)
+    where = [jnp.dot(((dev8 == dev_u) & (copy_rank == k)).astype(bf16), unit_exp, preferred_element_type=f32).astype(bf16) for k in range(n_copy)]
 
     for k in range(1, n_dev):
         src = lax.rem(me + n_dev - k, n_dev)
         pltpu.make_async_remote_copy(src_ref=hsend, dst_ref=hall.at[src], send_sem=ssem.at[k], recv_sem=rsem.at[k], device_id={'ep': src}, device_id_type=MESH).wait_recv()
-    every = jnp.concatenate([hall[p, 0:1, :] for p in range(n_dev)], axis=0)
-    loads, starts = slot_loads(every.astype(f32))
-    meta[0:n_dev, :] = loads
-    meta[n_dev:2 * n_dev, :] = starts
+    every = jnp.concatenate([hall[p, 0:1, :] for p in range(n_dev)], axis=0).astype(f32)
+    taken = level_copies(every, where, copies, float(bound))
+    loads = jnp.zeros((n_dev, n_units), f32)
+    cum = jnp.zeros((n_dev, LANES), f32)
+    for k in range(n_copy):
+        per_unit = lax.dot_general(taken[k].astype(bf16), unit_exp, nt, preferred_element_type=f32)
+        loads = jnp.where(copy_rank == k, per_unit, loads)
+        cums[k * n_dev:(k + 1) * n_dev, :] = cum
+        cum = cum + taken[k]
+    starts = jnp.dot(loads.astype(bf16), before, preferred_element_type=f32)
+    meta[0:n_dev, :] = loads.astype(i32)
+    meta[n_dev:2 * n_dev, :] = starts.astype(i32)
+
+    block = lax.rem(dev_u + n_dev - me, n_dev)
+    first = meta[pl.ds(n_dev + me, 1), :] + block * stride
+    row8 = lax.broadcasted_iota(i32, (2 * n_copy, n_units), 0)
+    half = jnp.where(row8 < n_copy, lax.shift_right_logical(first, 6), first & 63)
+    half = jnp.where(copy_rank == (row8 & (n_copy - 1)), half, 0)
+    place = jnp.dot(half.astype(bf16), unit_exp, preferred_element_type=f32).astype(i32)
+    own = [cums[pl.ds(k * n_dev + me, 1), :].astype(i32) for k in range(n_copy)]
+    offs = [place[k:k + 1] * 64 + place[n_copy + k:n_copy + k + 1] - own[k] + 256 for k in range(n_copy)]
+    bar = [jnp.where(copies > k, own[k], 255) for k in range(1, n_copy)]
+    rows = [lax.shift_right_logical(o, 6) for o in offs] + [o & 63 for o in offs] + bar + [jnp.zeros((1, LANES), i32)] * 5
+    lookup = jnp.concatenate(rows, axis=0).astype(f32).astype(bf16)
+
+    @pl.loop(0, n_rows // SUB)
+    def _(g):
+        base = pl.multiple_of(g * SUB, SUB)
+        ids = idx[pl.ds(base, SUB), :]
+        ranks = addr[pl.ds(base, SUB), :]
+        parts = []
+        for r in range(SUB):
+            rank = ranks[r:r + 1, :]
+            hot_b = (sub_e == ids[r:r + 1, :]).astype(bf16)
+            got = jnp.dot(lookup, hot_b, preferred_element_type=f32).astype(i32)
+            pos = got[0:1] * 64 + got[n_copy:n_copy + 1]
+            for k in range(1, n_copy):
+                pos = jnp.where(rank >= got[2 * n_copy + k - 1:2 * n_copy + k], got[k:k + 1] * 64 + got[n_copy + k:n_copy + k + 1], pos)
+            pos = pos + rank - 256
+            parts.append(pos + lax.shift_right_logical(pos, 3) * 40)
+        addr[pl.ds(base, SUB), :] = jnp.concatenate(parts, axis=0)
+
     slot_id = lane_u & (USTRIDE - 1)
-    low = jnp.zeros((1, n_units), i32)
-    high = jnp.zeros((1, n_units), i32)
+    lo_row = jnp.zeros((1, n_units), f32)
+    hi_row = jnp.zeros((1, n_units), f32)
     for s in range(n_slot):
-        low = jnp.where(slot_id == s, lo_bound[s], low)
-        high = jnp.where(slot_id == s, hi_bound[s], high)
+        lo_row = jnp.where(slot_id == s, float(low[s]), lo_row)
+        hi_row = jnp.where(slot_id == s, float(high[s]), hi_row)
     ends = loads + starts
-    bad = jnp.where(valid & ((ends < low) | (ends > high)), 1.0, 0.0)
-    flag[...] = jnp.broadcast_to(jnp.max(jnp.max(bad, axis=1, keepdims=True), axis=0, keepdims=True), flag.shape).astype(i32)
+    bad = jnp.max(jnp.where(valid & ((ends < lo_row) | (ends > hi_row)), 1.0, 0.0))
+    top = jnp.max(jnp.where(valid, ends, 0.0))
+    tier = jnp.where(bad > 0.0, float(len(caps)), sum(jnp.where(top > float(c), 1.0, 0.0) for c in caps))
+    flag[0, 0] = tier.astype(i32)
     for copy in sends:
         copy.wait_send()
 
 
-def pack_kernel(cap, addr, flag, tok_hbm, send, tok, wide, tmp, stage, tsem, ssem):
+def pack_kernel(cap, slow, addr, flag, tok_hbm, send, tok, wide, tmp, stage, tsem, ssem):
     n_rows, n_col = addr.shape
     n_dev, stride = stage.shape[0], stage.shape[1]
     d_tiles = tok.shape[1] // LANES
@@ -177,7 +230,7 @@
     def _(k):
         store(k, 0, cap).wait()
 
-    @pl.when(flag[0, 0] != 0)
+    @pl.when(flag[0, 0] == slow)
     def _():
         @pl.loop(0, n_dev)
         def _(k):
@@ -190,7 +243,7 @@
             rest.wait()
 
 
-def unpack_kernel(cap, addr, flag, gate, back_hbm, out_hbm, back, wide, tmp, out, bsem, osem):
+def unpack_kernel(cap, slow, addr, flag, gate, back_hbm, out_hbm, back, wide, tmp, out, bsem, osem):
     n_rows, n_col = addr.shape
     n_dev, stride = back.shape[0], back.shape[1]
     d_tiles = out.shape[1] // LANES
@@ -219,7 +272,7 @@
         def _(b):
             widen(k, b)
 
-    @pl.when(flag[0, 0] != 0)
+    @pl.when(flag[0, 0] == slow)
     def _():
         @pl.loop(0, n_dev)
         def _(k):
@@ -263,8 +316,7 @@
     n_dev, n_slot, part = cfg['n_dev'], cfg['n_slot'], cfg['part']
     m_rows = n_dev * part
     d_model, d_ff = up_hbm.shape[1], up_hbm.shape[2]
-    last, disp, ret, ret_lo = cfg['last'], cfg['disp'], cfg['ret'], cfg['ret_lo']
-    n_grp = len(last)
+    first, last, disp, ret, ret_lo = cfg['first'], cfg['last'], cfg['disp'], cfg['ret'], cfg['ret_lo']
     f32, bf16, i32 = jnp.float32, jnp.bfloat16, jnp.int32
     me = lax.axis_index('ep')
 
@@ -282,7 +334,7 @@
         return pltpu.make_async_copy(send.at[0, rows], recv.at[0, rows], drecv.at[j, 0])
 
     order = sorted(range(1, n_dev), key=lambda k: (abs(k - n_dev // 2), k))
-    for j in range(n_grp):
+    for j in range(len(first)):
         for k in order:
             dispatch(j, k, lax.rem(me + k, n_dev)).start()
         dispatch_own(j).start()
@@ -365,8 +417,8 @@
 
     @pl.loop(0, n_slot)
     def _(s):
-        for j in range(n_grp):
-            @pl.when(s == (0 if j == 0 else last[j - 1] + 1))
+        for j in range(len(first)):
+            @pl.when(s == first[j])
             def _():
                 for k in range(1, n_dev):
                     dispatch(j, k, lax.rem(me + n_dev - k, n_dev)).wait_recv()
@@ -388,38 +440,34 @@
             for copy in fetch(s + 2, b):
                 copy.start()
 
-        for j in range(n_grp):
+        for j in range(len(last)):
             @pl.when(s == last[j])
             def _():
                 combine(j)
 
-    for j in range(n_grp):
-        for k in range(1, n_dev):
+    for k in range(1, n_dev):
+        for j in range(len(first)):
             dispatch(j, k, lax.rem(me + k, n_dev)).wait_send()
+        for j in range(len(last)):
             give_back(j, k).wait_send()
             give_back(j, k).wait_recv()
+    for j in range(len(last)):
         give_own(j).wait()
 
 
-def plan(n_dev, n_slot, n_pairs, bound, z, z_cap, lasts):
-    stride = up_to(n_slot * bound, PACK)
+def plan(n_dev, n_slot, n_pairs, bound, z, cap, groups, returns):
     mean = n_pairs / (n_dev * n_slot)
     spread = 9.3 * mean / 30.1
-    if z is None:
-        hi = [bound * (s + 1) for s in range(n_slot)]
-        lo = [0] * n_slot
-    else:
-        hi = [min(bound * (s + 1), math.ceil(mean * (s + 1) + z * spread * math.sqrt(s + 1))) for s in range(n_slot)]
-        lo = [max(0, math.floor(mean * (s + 1) - z * spread * math.sqrt(s + 1))) for s in range(n_slot)]
-        lo[-1] = 0
-    cap = stride if z is None else min(stride, up_to(math.ceil(mean * n_slot + z_cap * spread * math.sqrt(n_slot)), PACK))
-    hi = [min(h, cap) for h in hi]
-    disp = [0] + [up_to(hi[s], PACK) for s in lasts]
-    disp = [min(d, cap) for d in disp[:-1]] + [cap]
-    ret = [0] + [lo[s] // PACK * PACK for s in lasts]
-    ret[-1] = cap
-    ret_lo = [min(s for s in range(n_slot) if hi[s] > ret[j]) for j in range(len(lasts))]
-    return dict(n_dev=n_dev, n_slot=n_slot, cap=cap, stride=stride, lo=lo, hi=hi, last=list(lasts), disp=disp, ret=ret, ret_lo=ret_lo, part=up_to(bound, PACK))
+    hi = [bound * (s + 1) for s in range(n_slot)]
+    lo = [0] * n_slot
+    if z is not None:
+        hi = [min(hi[s], math.ceil(mean * (s + 1) + z * spread * math.sqrt(s + 1)), cap) for s in range(n_slot)]
+        lo = [max(0, math.floor(mean * (s + 1) - z * spread * math.sqrt(s + 1))) for s in range(n_slot - 1)] + [0]
+    disp = [0] + [min(cap, up_to(hi[s], PACK)) for s in groups[:-1]] + [cap]
+    ret = [0] + [lo[s] // PACK * PACK for s in returns[:-1]] + [cap]
+    ret_lo = [min(s for s in range(n_slot) if hi[s] > ret[j]) for j in range(len(returns))]
+    first = [0] + [s + 1 for s in groups[:-1]]
+    return dict(n_dev=n_dev, n_slot=n_slot, cap=cap, lo=lo, hi=hi, first=first, last=list(returns), disp=disp, ret=ret, ret_lo=ret_lo, part=up_to(bound, PACK))
 
 
 def solution(mesh):
@@ -432,9 +480,13 @@
         n_pairs = n_tok * topk_idx.shape[1]
         base_load = n_pairs // (n_dev * n_slot)
         bound = base_load + base_load // 2 + 1
-        fast = plan(n_dev, n_slot, n_pairs, bound, 3.6, 2.9, [n_slot * 4 // 17 - 1, n_slot * 8 // 17 - 1, n_slot * 12 // 17 - 1, n_slot * 15 // 17 - 1, n_slot - 1])
-        slow = plan(n_dev, n_slot, n_pairs, bound, None, None, [n_slot - 1])
-        stride = fast['stride']
+        mean = n_pairs // n_dev
+        stride = up_to(n_slot * bound, PACK)
+        caps = [min(stride, up_to(math.ceil(mean * f), PACK)) for f in TIERS]
+        cuts = [n_slot * c // 17 - 1 for c in (4, 8, 12, 15, 17)]
+        plans = [plan(n_dev, n_slot, n_pairs, bound, 4.0, c, cuts[:3] + cuts[4:], cuts) for c in caps]
+        plans.append(plan(n_dev, n_slot, n_pairs, bound, None, stride, [n_slot - 1], [n_slot - 1]))
+        wide_bounds = plan(n_dev, n_slot, n_pairs, bound, 4.0, stride, cuts, cuts)
         n_rows = n_pairs // LANES
         n_units = n_dev * USTRIDE
         f32, bf16, i32 = jnp.float32, jnp.bfloat16, jnp.int32
@@ -444,11 +496,11 @@
         big = 63 * 1024 * 1024
 
         addr, meta, flag = pl.pallas_call(
-            functools.partial(route_kernel, n_dev, n_slot, stride, fast['lo'], fast['hi']),
-            out_shape=[jax.ShapeDtypeStruct((n_rows, LANES), i32), jax.ShapeDtypeStruct((2 * n_dev, n_units), i32), jax.ShapeDtypeStruct((SUB, LANES), i32)],
+            functools.partial(route_kernel, n_dev, n_slot, stride, bound, wide_bounds['lo'], wide_bounds['hi'], caps),
+            out_shape=[jax.ShapeDtypeStruct((n_rows, LANES), i32), jax.ShapeDtypeStruct((2 * n_dev, n_units), i32), jax.ShapeDtypeStruct((1, 1), i32)],
             in_specs=[vmem, smem],
-            out_specs=[vmem, vmem, vmem],
-            scratch_shapes=[pltpu.VMEM((SUB, LANES), i32), pltpu.VMEM((n_dev, SUB, LANES), i32), pltpu.VMEM((n_units, LANES), i32), pltpu.SemaphoreType.DMA((n_dev,)), pltpu.SemaphoreType.DMA((n_dev,))],
+            out_specs=[vmem, vmem, smem],
+            scratch_shapes=[pltpu.VMEM((SUB, LANES), i32), pltpu.VMEM((n_dev, SUB, LANES), i32), pltpu.VMEM((n_rows, LANES), f32), pltpu.VMEM((n_units, LANES), i32), pltpu.VMEM((4 * n_dev, LANES), f32), pltpu.SemaphoreType.DMA((n_dev,)), pltpu.SemaphoreType.DMA((n_dev,))],
             compiler_params=pltpu.CompilerParams(collective_id=0, has_side_effects=True),
             name='route',
         )(topk_idx.reshape(n_rows, LANES), slot_expert)
@@ -460,7 +512,7 @@
         rows_vmem = pltpu.VMEM((n_tok, d_model), bf16)
         sem, sems = pltpu.SemaphoreType.DMA, pltpu.SemaphoreType.DMA((n_dev,))
         send = pl.pallas_call(
-            functools.partial(pack_kernel, fast['cap']),
+            functools.partial(pack_kernel, caps[-1], len(caps)),
             out_shape=jax.ShapeDtypeStruct((n_dev, stride, d_model), bf16),
             in_specs=[smem, smem, hbm],
             out_specs=hbm,
@@ -470,10 +522,10 @@
         )(addr, flag, tokens)
 
         def run(cfg, meta, send, w_up, w_down):
-            n_grp = len(cfg['last'])
             part, cap = cfg['part'], cfg['cap']
             m_rows = n_dev * part
-            dma = pltpu.SemaphoreType.DMA((n_grp, n_dev))
+            sent = pltpu.SemaphoreType.DMA((len(cfg['first']), n_dev))
+            given = pltpu.SemaphoreType.DMA((len(cfg['last']), n_dev))
             return pl.pallas_call(
                 functools.partial(expert_kernel, cfg),
                 out_shape=jax.ShapeDtypeStruct((n_dev, stride, d_model), bf16),
@@ -488,17 +540,17 @@
                     pltpu.VMEM((m_rows, d_ff), bf16),
                     pltpu.VMEM((m_rows, d_model), bf16),
                     pltpu.VMEM((n_dev * WIN, d_model), bf16),
-                    dma, dma, dma, dma,
+                    sent, sent, given, given,
                     pltpu.SemaphoreType.DMA((2, 2)),
                 ],
                 compiler_params=pltpu.CompilerParams(collective_id=1, has_side_effects=True, vmem_limit_bytes=big),
                 name='experts',
             )(meta, send, w_up, w_down)
 
-        back = lax.cond(flag[0, 0] == 0, functools.partial(run, fast), functools.partial(run, slow), meta, send, w_up[0], w_down[0])
+        back = lax.switch(flag[0, 0], [functools.partial(run, p) for p in plans], meta, send, w_up[0], w_down[0])
 
         return pl.pallas_call(
-            functools.partial(unpack_kernel, fast['cap']),
+            functools.partial(unpack_kernel, caps[-1], len(caps)),
             out_shape=jax.ShapeDtypeStruct((n_tok, d_model), bf16),
             in_specs=[smem, smem, smem, hbm],
             out_specs=hbm,

time: 214 us -> 205 us (0.958)
  Pallas kernels: 211 us -> 201 us
    pallas_call x1, Pallas kernels: 171 us -> 161 us  [run(): pl.pallas_call(functools.partial(expert_kernel, cfg), out_shape=jax.Shape...]
where the time goes in v3:
time: 205 us; the launch traced here: 203 us
  Pallas kernels  201 us (98%)
    pallas_call x1, Pallas kernels, run(): pl.pallas_call(functools.partial(expert_kernel, cfg), out_shape=jax.Shape...  161 us
    pallas_call x1, Pallas kernels, group_layer(): pl.pallas_call(functools.partial(unpack_kernel, caps[-1], len(caps)), out...  14.4 us
    pallas_call x1, Pallas kernels, group_layer(): pl.pallas_call(functools.partial(pack_kernel, caps[-1], len(caps)), out_s...  13.8 us
    pallas_call x1, Pallas kernels, group_layer(): pl.pallas_call(functools.partial(route_kernel, n_dev, n_slot, stride, bou...  12 us

profile of v3, /device:TPU:113, one launch (start us, length us, event | category | flops | bytes accessed | tf_op | source)
XLA Modules:
  0.0 203.1 jit_solution(16922543604107210004)
XLA Ops:
  0.0 12.0 %route.1 = (s32[32,128]{1,0:T(8,128)}, s32[16,256]{1,0:T(8,128)S(1)}, s32[1,1]{1,0:T(1,128)}) custom-call(s32[32,128]{1,0:T(8,128)} %bitcast.6, s32[8,17]{1,0:T(8,128)} %table.1), custom_call_target="tpu_custom_call" | custom-call | tf_op jit(solution)/shard_map/route/pallas_call | solution.py:498
  12.6 13.8 %pack.1 = bf16[8,784,768]{2,1,0:T(8,128)(2,1)} custom-call(s32[32,128]{1,0:T(8,128)} %get-tuple-element.74.addr, s32[1,1]{1,0:T(1,128)} %get-tuple-element.75.flag, bf16[4096,768]{1,0:T(8,128)(2,1)} %tok_hbm.1), custom_call_target="tpu_custom_call" | custom-call | tf_op jit(solution)/shard_map/pack/pallas_call | solution.py:514
  26.5 161.9 %conditional.1 = (bf16[8,784,768]{2,1,0:T(8,128)(2,1)}) conditional(s32[]{:T(128)} %bitcast.2, (s32[16,256]{1,0:T(8,128)S(1)}, bf16[8,784,768]{2,1,0:T(8,128)(2,1)}, bf16[17,768,3072]{2,1,0:T(8,128)(2,1)}, bf16[17,3072,768]{2,1,0:T(8,128)(2,1)}) %tuple.20, (s32[16,256]{1,0:T(8,128)S(1)}, ...), branch_computations={%region_0.0_spmd, %region_1.0_spmd, %region_2.0_spmd, %region_3.0_... | conditional | bytes 8 | solution.py:550
  26.5 161.2 %experts.5 = bf16[8,784,768]{2,1,0:T(8,128)(2,1)} custom-call(s32[16,256]{1,0:T(8,128)S(1)} %get-tuple-element.44.meta, bf16[8,784,768]{2,1,0:T(8,128)(2,1)} %get-tuple-element.50.send, bf16[17,768,3072]{2,1,0:T(8,128)(2,1)} %get-tuple-element.52.up_hbm, bf16[17,3072,768]{2,1,0:T(8,128)(2,1)} %get-tuple-element.54.down_hbm), custom_call_target="tpu_custom_call" | custom-call | tf_op jit(solution)/shard_map/cond/branch_0_fun/experts/pallas_call | solution.py:529
  188.4 14.4 %unpack.1 = bf16[4096,768]{1,0:T(8,128)(2,1)} custom-call(s32[32,128]{1,0:T(8,128)} %get-tuple-element.74.addr, s32[1,1]{1,0:T(1,128)} %get-tuple-element.75.flag, f32[32,128]{1,0:T(8,128)} %bitcast.5, bf16[8,784,768]{2,1,0:T(8,128)(2,1)} %get-tuple-element.77.back_hbm), custom_call_target="tpu_custom_call" | custom-call | tf_op jit(solution)/shard_map/unpack/pallas_call | solution.py:552

commit v4 on v3

--- a/solution.py
+++ b/solution.py
@@ -14,7 +14,9 @@
 PACK = 16
 USTRIDE = 32
 WIN = 64
-TIERS = (1.125, 1.156, 1.1875, 1.25)
+STEP = 32
+CHUNK = 128
+TIERS = (1.125, 1.156, 1.21875)
 
 
 def up_to(x, m):
@@ -180,83 +182,20 @@
         copy.wait_send()
 
 
-def pack_kernel(cap, slow, addr, flag, tok_hbm, send, tok, wide, tmp, stage, tsem, ssem):
-    n_rows, n_col = addr.shape
-    n_dev, stride = stage.shape[0], stage.shape[1]
-    d_tiles = tok.shape[1] // LANES
-    step = SUB * d_tiles
-    load = pltpu.make_async_copy(tok_hbm, tok, tsem)
-    load.start()
-    zero_rows = 4 * step
-
-    @pl.loop(0, wide.shape[0] // zero_rows)
-    def _(b):
-        wide[pl.ds(pl.multiple_of(b * zero_rows, zero_rows), zero_rows), :] = jnp.zeros((zero_rows, LANES), jnp.float32)
-
-    load.wait()
-
-    @pl.loop(0, n_rows)
-    def _(r):
-        for c in range(n_col // PACK):
-            at = c * 2 * step
-            x = tok[pl.ds(pl.multiple_of(r * n_col + c * PACK, PACK), PACK), :].astype(jnp.float32)
-            for h in range(PACK // SUB):
-                for j in range(d_tiles):
-                    tmp[at + h * step + j * SUB:at + h * step + (j + 1) * SUB, :] = x[h * SUB:(h + 1) * SUB, j * LANES:(j + 1) * LANES]
-            for i in range(PACK):
-                a = addr[r, c * PACK + i]
-                wide[pl.ds(a, d_tiles, stride=SUB), :] = tmp[pl.ds(at + (i // SUB) * step + i % SUB, d_tiles, stride=SUB), :]
-
-    def narrow(k, b):
-        base = (k * (stride // PACK) + b) * (2 * step)
-        rows = pl.ds(pl.multiple_of(b * PACK, PACK), PACK)
-        for j in range(d_tiles):
-            top = wide[pl.ds(base + j * SUB, SUB), :]
-            bot = wide[pl.ds(base + step + j * SUB, SUB), :]
-            stage[k, rows, j * LANES:(j + 1) * LANES] = jnp.concatenate([top, bot], axis=0).astype(jnp.bfloat16)
-
-    def store(k, lo, hi):
-        return pltpu.make_async_copy(stage.at[k, pl.ds(lo, hi - lo)], send.at[k, pl.ds(lo, hi - lo)], ssem.at[k])
-
-    @pl.loop(0, n_dev)
-    def _(k):
-        @pl.loop(0, cap // PACK, unroll=4)
-        def _(b):
-            narrow(k, b)
-
-        store(k, 0, cap).start()
-
-    @pl.loop(0, n_dev)
-    def _(k):
-        store(k, 0, cap).wait()
-
-    @pl.when(flag[0, 0] == slow)
-    def _():
-        @pl.loop(0, n_dev)
-        def _(k):
-            @pl.loop(cap // PACK, stride // PACK)
-            def _(b):
-                narrow(k, b)
-
-            rest = store(k, cap, stride)
-            rest.start()
-            rest.wait()
-
-
 def unpack_kernel(cap, slow, addr, flag, gate, back_hbm, out_hbm, back, wide, tmp, out, bsem, osem):
     n_rows, n_col = addr.shape
-    n_dev, stride = back.shape[0], back.shape[1]
+    n_dev, stride = back.shape[0], back.shape[1] * PACK
     d_tiles = out.shape[1] // LANES
     step = SUB * d_tiles
 
     def load(k, lo, hi):
-        return pltpu.make_async_copy(back_hbm.at[k, pl.ds(lo, hi - lo)], back.at[k, pl.ds(lo, hi - lo)], bsem.at[k])
+        rows = pl.ds(lo // PACK, (hi - lo) // PACK)
+        return pltpu.make_async_copy(back_hbm.at[k, rows], back.at[k, rows], bsem.at[k])
 
     def widen(k, b):
         base = (k * (stride // PACK) + b) * (2 * step)
-        rows = pl.ds(pl.multiple_of(b * PACK, PACK), PACK)
         for j in range(d_tiles):
-            x = back[k, rows, j * LANES:(j + 1) * LANES].astype(jnp.float32)
+            x = back[k, b, :, j * LANES:(j + 1) * LANES].astype(jnp.float32)
             wide[pl.ds(base + j * SUB, SUB), :] = x[:SUB]
             wide[pl.ds(base + step + j * SUB, SUB), :] = x[SUB:]
 
@@ -312,42 +251,67 @@
     return x * (0.5 * (1.0 + jnp.tanh(0.7978845608028654 * (x + 0.044715 * (x * x * x)))))
 
 
-def expert_kernel(cfg, meta, send, up_hbm, down_hbm, back, recv, xbuf, ybuf, up, down, hid, xs, win, dsend, drecv, rsend, rrecv, wsem):
-    n_dev, n_slot, part = cfg['n_dev'], cfg['n_slot'], cfg['part']
+def expert_kernel(cfg, meta, addr, tok_hbm, up_hbm, down_hbm, back, tok, recv, xbuf, ybuf, up, down, mix, xs, win, dsend, drecv, rsend, rrecv, wsem, tsem):
+    n_dev, n_slot, part, stride = cfg['n_dev'], cfg['n_slot'], cfg['part'], cfg['stride']
     m_rows = n_dev * part
-    d_model, d_ff = up_hbm.shape[1], up_hbm.shape[2]
+    n_tok, d_model, d_ff = tok.shape[0], up_hbm.shape[1], up_hbm.shape[2]
     first, last, disp, ret, ret_lo = cfg['first'], cfg['last'], cfg['disp'], cfg['ret'], cfg['ret_lo']
+    n_step = -(-disp[-1] // STEP)
     f32, bf16, i32 = jnp.float32, jnp.bfloat16, jnp.int32
     me = lax.axis_index('ep')
 
     def fetch(s, b):
         return (pltpu.make_async_copy(up_hbm.at[s], up.at[b], wsem.at[0, b]), pltpu.make_async_copy(down_hbm.at[s], down.at[b], wsem.at[1, b]))
 
+    load_tok = pltpu.make_async_copy(tok_hbm, tok, tsem)
+    load_tok.start()
     group_barrier(n_dev, me)
-
-    def dispatch(j, k, peer):
-        rows = pl.ds(disp[j], disp[j + 1] - disp[j])
-        return pltpu.make_async_remote_copy(src_ref=send.at[k, rows], dst_ref=recv.at[k, rows], send_sem=dsend.at[j, k], recv_sem=drecv.at[j, k], device_id={'ep': peer}, device_id_type=MESH)
-
-    def dispatch_own(j):
-        rows = pl.ds(disp[j], disp[j + 1] - disp[j])
-        return pltpu.make_async_copy(send.at[0, rows], recv.at[0, rows], drecv.at[j, 0])
+    tail = n_step * (STEP // PACK)
+
+    @pl.loop(0, n_dev)
+    def _(k):
+        xbuf[k, tail:] = jnp.zeros((xbuf.shape[1] - tail, PACK, d_model), bf16)
+
+    def dispatch(j, k, peer, lo, num):
+        return pltpu.make_async_remote_copy(src_ref=xbuf.at[k, pl.ds(lo, num)], dst_ref=recv.at[k, pl.ds(lo, num)], send_sem=dsend.at[j, k], recv_sem=drecv.at[j, k], device_id={'ep': peer}, device_id_type=MESH)
+
+    def dispatched(j, k, peer):
+        return dispatch(j, k, peer, disp[j] // PACK, (disp[j + 1] - disp[j]) // PACK)
 
     order = sorted(range(1, n_dev), key=lambda k: (abs(k - n_dev // 2), k))
-    for j in range(len(first)):
-        for k in order:
-            dispatch(j, k, lax.rem(me + k, n_dev)).start()
-        dispatch_own(j).start()
-        if j == 0:
+    whole = disp[-1] // STEP
+    load_tok.wait()
+
+    @pl.loop(0, n_step)
+    def _(u):
+        row = lax.broadcasted_iota(i32, (n_dev * STEP, LANES), 0)
+        pos = lax.shift_right_logical(row, 5) * stride + (row & (STEP - 1)) + u * STEP
+        want = pos + lax.shift_right_logical(pos, 3) * 40
+        for q in range(n_tok // LANES):
+            mix[:n_dev * STEP, q * LANES:(q + 1) * LANES] = (want == addr[q:q + 1, :]).astype(bf16)
+        rows = jnp.dot(mix[:n_dev * STEP, :n_tok], tok[...], preferred_element_type=f32).astype(bf16)
+        for k in range(n_dev):
+            for h in range(STEP // PACK):
+                at = k * STEP + h * PACK
+                xbuf[k, u * (STEP // PACK) + h] = rows[at:at + PACK]
+        j = u // (CHUNK // STEP) if len(first) > 1 else 0
+
+        @pl.when(u < whole)
+        def _():
+            for k in order:
+                dispatch(j, k, lax.rem(me + k, n_dev), u * (STEP // PACK), STEP // PACK).start()
+
+        if whole < n_step:
+            @pl.when(u == whole)
+            def _():
+                for k in order:
+                    dispatch(j, k, lax.rem(me + k, n_dev), u * (STEP // PACK), (disp[-1] - whole * STEP) // PACK).start()
+
+        @pl.when(u == 0)
+        def _():
             for s in range(2):
                 for copy in fetch(s, s):
                     copy.start()
-
-    @pl.loop(0, n_dev)
-    def _(k):
-        @pl.loop(0, xbuf.shape[1])
-        def _(b):
-            xbuf[k, b] = jnp.zeros((PACK, d_model), bf16)
 
     def ffn(s, b):
         unit = me * USTRIDE + s
@@ -371,20 +335,20 @@
         tile = 512
         for t in range(d_ff // tile):
             pre = jnp.dot(xs[...], up[b, :, t * tile:(t + 1) * tile], preferred_element_type=f32)
-            hid[:, t * tile:(t + 1) * tile] = gelu(pre).astype(bf16)
+            mix[:, t * tile:(t + 1) * tile] = gelu(pre).astype(bf16)
         tile = 256
         for t in range(d_model // tile):
-            o = jnp.dot(hid[...], down[b, :, t * tile:(t + 1) * tile], preferred_element_type=f32).astype(bf16)
+            o = jnp.dot(mix[:, :d_ff], down[b, :, t * tile:(t + 1) * tile], preferred_element_type=f32).astype(bf16)
             for k in range(n_dev):
                 ybuf[k, pl.ds(pl.multiple_of(s * part, PACK), part), t * tile:(t + 1) * tile] = o[k * part:(k + 1) * part]
 
     def give_back(j, k):
-        rows = pl.ds(ret[j], ret[j + 1] - ret[j])
+        rows = pl.ds(ret[j] // PACK, (ret[j + 1] - ret[j]) // PACK)
         peer = lax.rem(me + n_dev - k, n_dev)
         return pltpu.make_async_remote_copy(src_ref=recv.at[k, rows], dst_ref=back.at[k, rows], send_sem=rsend.at[j, k], recv_sem=rrecv.at[j, k], device_id={'ep': peer}, device_id_type=MESH)
 
     def give_own(j):
-        rows = pl.ds(ret[j], ret[j + 1] - ret[j])
+        rows = pl.ds(ret[j] // PACK, (ret[j + 1] - ret[j]) // PACK)
         return pltpu.make_async_copy(recv.at[0, rows], back.at[0, rows], rrecv.at[j, 0])
 
     def combine(j):
@@ -405,7 +369,8 @@
                 target = jnp.where((nth >= 0) & (nth < load), nth + start, target)
             pick = (lax.broadcasted_iota(i32, (n_rows, width), 0) + ret[j] == target).astype(bf16)
             rows = ybuf[k, ret_lo[j] * part:(last[j] + 1) * part, :]
-            recv[k, ret[j]:ret[j + 1], :] = jnp.dot(pick, rows, preferred_element_type=f32).astype(bf16)
+            mixed = jnp.dot(pick, rows, preferred_element_type=f32).astype(bf16)
+            recv[k, ret[j] // PACK:ret[j + 1] // PACK] = mixed.reshape(n_rows // PACK, PACK, d_model)
 
             @pl.when(k == 0)
             def _():
@@ -421,14 +386,14 @@
             @pl.when(s == first[j])
             def _():
                 for k in range(1, n_dev):
-                    dispatch(j, k, lax.rem(me + n_dev - k, n_dev)).wait_recv()
-                dispatch_own(j).wait()
-
-                @pl.loop(0, n_dev)
+                    dispatched(j, k, lax.rem(me + n_dev - k, n_dev)).wait_recv()
+                    dispatched(j, k, lax.rem(me + k, n_dev)).wait_send()
+
+                @pl.loop(1, n_dev)
                 def _(k):
                     @pl.loop(disp[j] // PACK, disp[j + 1] // PACK)
                     def _(b):
-                        xbuf[k, b] = recv[k, pl.ds(pl.multiple_of(b * PACK, PACK), PACK), :]
+                        xbuf[k, b] = recv[k, b]
 
         b = lax.rem(s, 2)
         for copy in fetch(s, b):
@@ -446,8 +411,6 @@
                 combine(j)
 
     for k in range(1, n_dev):
-        for j in range(len(first)):
-            dispatch(j, k, lax.rem(me + k, n_dev)).wait_send()
         for j in range(len(last)):
             give_back(j, k).wait_send()
             give_back(j, k).wait_recv()
@@ -455,7 +418,7 @@
         give_own(j).wait()
 
 
-def plan(n_dev, n_slot, n_pairs, bound, z, cap, groups, returns):
+def plan(n_dev, n_slot, n_pairs, bound, stride, z, cap, returns):
     mean = n_pairs / (n_dev * n_slot)
     spread = 9.3 * mean / 30.1
     hi = [bound * (s + 1) for s in range(n_slot)]
@@ -463,11 +426,11 @@
     if z is not None:
         hi = [min(hi[s], math.ceil(mean * (s + 1) + z * spread * math.sqrt(s + 1)), cap) for s in range(n_slot)]
         lo = [max(0, math.floor(mean * (s + 1) - z * spread * math.sqrt(s + 1))) for s in range(n_slot - 1)] + [0]
-    disp = [0] + [min(cap, up_to(hi[s], PACK)) for s in groups[:-1]] + [cap]
+    disp = [0, cap] if z is None else list(range(0, cap, CHUNK)) + [cap]
     ret = [0] + [lo[s] // PACK * PACK for s in returns[:-1]] + [cap]
     ret_lo = [min(s for s in range(n_slot) if hi[s] > ret[j]) for j in range(len(returns))]
-    first = [0] + [s + 1 for s in groups[:-1]]
-    return dict(n_dev=n_dev, n_slot=n_slot, cap=cap, lo=lo, hi=hi, first=first, last=list(returns), disp=disp, ret=ret, ret_lo=ret_lo, part=up_to(bound, PACK))
+    first = [min((s for s in range(n_slot) if hi[s] > d), default=n_slot - 1) for d in disp[:-1]]
+    return dict(n_dev=n_dev, n_slot=n_slot, cap=cap, stride=stride, lo=lo, hi=hi, first=first, last=list(returns), disp=disp, ret=ret, ret_lo=ret_lo, part=up_to(bound, PACK))
 
 
 def solution(mesh):
@@ -483,10 +446,10 @@
         mean = n_pairs // n_dev
         stride = up_to(n_slot * bound, PACK)
         caps = [min(stride, up_to(math.ceil(mean * f), PACK)) for f in TIERS]
-        cuts = [n_slot * c // 17 - 1 for c in (4, 8, 12, 15, 17)]
-        plans = [plan(n_dev, n_slot, n_pairs, bound, 4.0, c, cuts[:3] + cuts[4:], cuts) for c in caps]
-        plans.append(plan(n_dev, n_slot, n_pairs, bound, None, stride, [n_slot - 1], [n_slot - 1]))
-        wide_bounds = plan(n_dev, n_slot, n_pairs, bound, 4.0, stride, cuts, cuts)
+        cuts = [n_slot * c // 17 - 1 for c in (5, 9, 12, 15, 17)]
+        plans = [plan(n_dev, n_slot, n_pairs, bound, stride, 4.0, c, cuts) for c in caps]
+        plans.append(plan(n_dev, n_slot, n_pairs, bound, stride, None, stride, [n_slot - 1]))
+        wide_bounds = plan(n_dev, n_slot, n_pairs, bound, stride, 4.0, stride, cuts)
         n_rows = n_pairs // LANES
         n_units = n_dev * USTRIDE
         f32, bf16, i32 = jnp.float32, jnp.bfloat16, jnp.int32
@@ -508,46 +471,38 @@
         d_tiles = d_model // LANES
         wide = pltpu.VMEM((n_dev * stride * d_tiles, LANES), f32)
         tmp = pltpu.VMEM((LANES * d_tiles, LANES), f32)
-        block = pltpu.VMEM((n_dev, stride, d_model), bf16)
+        block = pltpu.VMEM((n_dev, stride // PACK, PACK, d_model), bf16)
         rows_vmem = pltpu.VMEM((n_tok, d_model), bf16)
         sem, sems = pltpu.SemaphoreType.DMA, pltpu.SemaphoreType.DMA((n_dev,))
-        send = pl.pallas_call(
-            functools.partial(pack_kernel, caps[-1], len(caps)),
-            out_shape=jax.ShapeDtypeStruct((n_dev, stride, d_model), bf16),
-            in_specs=[smem, smem, hbm],
-            out_specs=hbm,
-            scratch_shapes=[rows_vmem, wide, tmp, block, sem, sems],
-            compiler_params=pltpu.CompilerParams(vmem_limit_bytes=big),
-            name='pack',
-        )(addr, flag, tokens)
-
-        def run(cfg, meta, send, w_up, w_down):
+        def run(cfg, meta, addr, tokens, w_up, w_down):
             part, cap = cfg['part'], cfg['cap']
             m_rows = n_dev * part
             sent = pltpu.SemaphoreType.DMA((len(cfg['first']), n_dev))
             given = pltpu.SemaphoreType.DMA((len(cfg['last']), n_dev))
             return pl.pallas_call(
                 functools.partial(expert_kernel, cfg),
-                out_shape=jax.ShapeDtypeStruct((n_dev, stride, d_model), bf16),
-                in_specs=[smem, hbm, hbm, hbm],
+                out_shape=jax.ShapeDtypeStruct((n_dev, stride // PACK, PACK, d_model), bf16),
+                in_specs=[smem, vmem, hbm, hbm, hbm],
                 out_specs=hbm,
                 scratch_shapes=[
-                    pltpu.VMEM((n_dev, cap, d_model), bf16),
-                    pltpu.VMEM((n_dev, (cap + WIN) // PACK, PACK, d_model), bf16),
+                    rows_vmem,
+                    pltpu.VMEM((n_dev, cap // PACK, PACK, d_model), bf16),
+                    pltpu.VMEM((n_dev, (up_to(cap, STEP) + WIN) // PACK, PACK, d_model), bf16),
                     pltpu.VMEM((n_dev, n_slot * part, d_model), bf16),
                     pltpu.VMEM((2, d_model, d_ff), bf16),
                     pltpu.VMEM((2, d_ff, d_model), bf16),
-                    pltpu.VMEM((m_rows, d_ff), bf16),
+                    pltpu.VMEM((m_rows, max(d_ff, n_tok)), bf16),
                     pltpu.VMEM((m_rows, d_model), bf16),
                     pltpu.VMEM((n_dev * WIN, d_model), bf16),
                     sent, sent, given, given,
                     pltpu.SemaphoreType.DMA((2, 2)),
+                    sem,
                 ],
                 compiler_params=pltpu.CompilerParams(collective_id=1, has_side_effects=True, vmem_limit_bytes=big),
                 name='experts',
-            )(meta, send, w_up, w_down)
-
-        back = lax.switch(flag[0, 0], [functools.partial(run, p) for p in plans], meta, send, w_up[0], w_down[0])
+            )(meta, addr, tokens, w_up, w_down)
+
+        back = lax.switch(flag[0, 0], [functools.partial(run, p) for p in plans], meta, addr, tokens, w_up[0], w_down[0])
 
         return pl.pallas_call(
             functools.partial(unpack_kernel, caps[-1], len(caps)),

time: 205 us -> 203 us (level)
    pallas_call x1 -> x0, Pallas kernels: 13.8 us -> none  [group_layer(): pl.pallas_call(functools.partial(pack_kernel, caps[-1], len(caps)), out_s...]
    pallas_call x1, Pallas kernels: 161 us -> 175 us  [run(): pl.pallas_call(functools.partial(expert_kernel, cfg), out_shape=jax.Shape...]
where the time goes in v4:
time: 203 us
  Pallas kernels  201 us (99%)
    pallas_call x1, Pallas kernels, run(): pl.pallas_call(functools.partial(expert_kernel, cfg), out_shape=jax.Shape...  175 us
    pallas_call x1, Pallas kernels, group_layer(): pl.pallas_call(functools.partial(unpack_kernel, caps[-1], len(caps)), out...  14.4 us
    pallas_call x1, Pallas kernels, group_layer(): pl.pallas_call(functools.partial(route_kernel, n_dev, n_slot, stride, bou...  11.9 us

profile of v4, /device:TPU:113, one launch (start us, length us, event | category | flops | bytes accessed | tf_op | source)
XLA Modules:
  0.0 202.8 jit_solution(8651511264050227662)
XLA Ops:
  0.0 11.9 %route.1 = (s32[32,128]{1,0:T(8,128)S(1)}, s32[16,256]{1,0:T(8,128)S(1)}, s32[1,1]{1,0:T(1,128)}) custom-call(s32[32,128]{1,0:T(8,128)} %bitcast.6, s32[8,17]{1,0:T(8,128)} %table.1), custom_call_target="tpu_custom_call" | custom-call | tf_op jit(solution)/shard_map/route/pallas_call | solution.py:461
  12.6 175.6 %conditional.1 = (bf16[8,49,16,768]{3,2,1,0:T(8,128)(2,1)}) conditional(s32[]{:T(128)} %bitcast.2, (s32[16,256]{1,0:T(8,128)S(1)}, s32[32,128]{1,0:T(8,128)S(1)}, bf16[4096,768]{1,0:T(8,128)(2,1)}, bf16[17,768,3072]{2,1,0:T(8,128)(2,1)}, bf16[17,3072,768]{2,1,0:T(8,128)(2,1)}) %tuple.17, (s32[16,256]{1,0:T(8,128)S(1)}, ...), branch_computations={%region_0.0_spmd, %region_1.0_spmd, %region_2.0_spmd, %region_3.0_... | conditional | bytes 8 | solution.py:505
  12.6 174.9 %experts.4 = bf16[8,49,16,768]{3,2,1,0:T(8,128)(2,1)} custom-call(s32[16,256]{1,0:T(8,128)S(1)} %get-tuple-element.48.meta, s32[32,128]{1,0:T(8,128)S(1)} %get-tuple-element.50.addr, bf16[4096,768]{1,0:T(8,128)(2,1)} %get-tuple-element.52.tok_hbm, bf16[17,768,3072]{2,1,0:T(8,128)(2,1)} %get-tuple-element.53.up_hbm, ...), custom_call_target="tpu_custom_call" | custom-call | tf_op jit(solution)/shard_map/cond/branch_0_fun/experts/pallas_call | solution.py:482
  188.2 14.4 %unpack.1 = bf16[4096,768]{1,0:T(8,128)(2,1)} custom-call(s32[32,128]{1,0:T(8,128)S(1)} %get-tuple-element.73.addr, s32[1,1]{1,0:T(1,128)} %get-tuple-element.74.flag, f32[32,128]{1,0:T(8,128)} %bitcast.5, bf16[8,49,16,768]{3,2,1,0:T(8,128)(2,1)} %get-tuple-element.76.back_hbm), custom_call_target="tpu_custom_call" | custom-call | tf_op jit(solution)/shard_map/unpack/pallas_call | solution.py:507

commit v5 on v4

--- a/solution.py
+++ b/solution.py
@@ -279,7 +279,6 @@
         return dispatch(j, k, peer, disp[j] // PACK, (disp[j + 1] - disp[j]) // PACK)
 
     order = sorted(range(1, n_dev), key=lambda k: (abs(k - n_dev // 2), k))
-    whole = disp[-1] // STEP
     load_tok.wait()
 
     @pl.loop(0, n_step)
@@ -294,18 +293,11 @@
             for h in range(STEP // PACK):
                 at = k * STEP + h * PACK
                 xbuf[k, u * (STEP // PACK) + h] = rows[at:at + PACK]
-        j = u // (CHUNK // STEP) if len(first) > 1 else 0
-
-        @pl.when(u < whole)
-        def _():
-            for k in order:
-                dispatch(j, k, lax.rem(me + k, n_dev), u * (STEP // PACK), STEP // PACK).start()
-
-        if whole < n_step:
-            @pl.when(u == whole)
+        for lo, hi, j in cfg['pieces']:
+            @pl.when(u == -(-hi // STEP) - 1)
             def _():
                 for k in order:
-                    dispatch(j, k, lax.rem(me + k, n_dev), u * (STEP // PACK), (disp[-1] - whole * STEP) // PACK).start()
+                    dispatch(j, k, lax.rem(me + k, n_dev), lo // PACK, (hi - lo) // PACK).start()
 
         @pl.when(u == 0)
         def _():
@@ -426,11 +418,13 @@
     if z is not None:
         hi = [min(hi[s], math.ceil(mean * (s + 1) + z * spread * math.sqrt(s + 1)), cap) for s in range(n_slot)]
         lo = [max(0, math.floor(mean * (s + 1) - z * spread * math.sqrt(s + 1))) for s in range(n_slot - 1)] + [0]
-    disp = [0, cap] if z is None else list(range(0, cap, CHUNK)) + [cap]
+    disp = [0, cap] if z is None else list(range(0, cap - CHUNK, CHUNK)) + [cap]
+    pieces = [(0, STEP, 0), (STEP, 2 * STEP, 0), (2 * STEP, disp[1], 0)]
+    pieces += [(disp[j], disp[j + 1], j) for j in range(1, len(disp) - 1)]
     ret = [0] + [lo[s] // PACK * PACK for s in returns[:-1]] + [cap]
     ret_lo = [min(s for s in range(n_slot) if hi[s] > ret[j]) for j in range(len(returns))]
     first = [min((s for s in range(n_slot) if hi[s] > d), default=n_slot - 1) for d in disp[:-1]]
-    return dict(n_dev=n_dev, n_slot=n_slot, cap=cap, stride=stride, lo=lo, hi=hi, first=first, last=list(returns), disp=disp, ret=ret, ret_lo=ret_lo, part=up_to(bound, PACK))
+    return dict(n_dev=n_dev, n_slot=n_slot, cap=cap, stride=stride, pieces=pieces, lo=lo, hi=hi, first=first, last=list(returns), disp=disp, ret=ret, ret_lo=ret_lo, part=up_to(bound, PACK))
 
 
 def solution(mesh):
@@ -446,7 +440,7 @@
         mean = n_pairs // n_dev
         stride = up_to(n_slot * bound, PACK)
         caps = [min(stride, up_to(math.ceil(mean * f), PACK)) for f in TIERS]
-        cuts = [n_slot * c // 17 - 1 for c in (5, 9, 12, 15, 17)]
+        cuts = [n_slot * c // 17 - 1 for c in (9, 12, 15, 17)]
         plans = [plan(n_dev, n_slot, n_pairs, bound, stride, 4.0, c, cuts) for c in caps]
         plans.append(plan(n_dev, n_slot, n_pairs, bound, stride, None, stride, [n_slot - 1]))
         wide_bounds = plan(n_dev, n_slot, n_pairs, bound, stride, 4.0, stride, cuts)

time: 203 us -> 203 us (level)
  no operation moved by 1% of the time
where the time goes in v5:
time: 203 us; the launch traced here: 204 us
  Pallas kernels  203 us (100%)
    pallas_call x1, Pallas kernels, run(): pl.pallas_call(functools.partial(expert_kernel, cfg), out_shape=jax.Shape...  177 us
    pallas_call x1, Pallas kernels, group_layer(): pl.pallas_call(functools.partial(unpack_kernel, caps[-1], len(caps)), out...  14.4 us
    pallas_call x1, Pallas kernels, group_layer(): pl.pallas_call(functools.partial(route_kernel, n_dev, n_slot, stride, bou...  11.9 us

profile of v5, /device:TPU:113, one launch (start us, length us, event | category | flops | bytes accessed | tf_op | source)
XLA Modules:
  0.0 204.5 jit_solution(6913255302012165895)
XLA Ops:
  0.0 11.9 %route.1 = (s32[32,128]{1,0:T(8,128)S(1)}, s32[16,256]{1,0:T(8,128)S(1)}, s32[1,1]{1,0:T(1,128)}) custom-call(s32[32,128]{1,0:T(8,128)} %bitcast.6, s32[8,17]{1,0:T(8,128)} %table.1), custom_call_target="tpu_custom_call" | custom-call | tf_op jit(solution)/shard_map/route/pallas_call | solution.py:455
  12.6 177.3 %conditional.1 = (bf16[8,49,16,768]{3,2,1,0:T(8,128)(2,1)}) conditional(s32[]{:T(128)} %bitcast.2, (s32[16,256]{1,0:T(8,128)S(1)}, s32[32,128]{1,0:T(8,128)S(1)}, bf16[4096,768]{1,0:T(8,128)(2,1)}, bf16[17,768,3072]{2,1,0:T(8,128)(2,1)}, bf16[17,3072,768]{2,1,0:T(8,128)(2,1)}) %tuple.17, (s32[16,256]{1,0:T(8,128)S(1)}, ...), branch_computations={%region_0.0_spmd, %region_1.0_spmd, %region_2.0_spmd, %region_3.0_... | conditional | bytes 8 | solution.py:499
  12.8 176.5 %experts.5 = bf16[8,49,16,768]{3,2,1,0:T(8,128)(2,1)} custom-call(s32[16,256]{1,0:T(8,128)S(1)} %get-tuple-element.55.meta, s32[32,128]{1,0:T(8,128)S(1)} %get-tuple-element.56.addr, bf16[4096,768]{1,0:T(8,128)(2,1)} %get-tuple-element.57.tok_hbm, bf16[17,768,3072]{2,1,0:T(8,128)(2,1)} %get-tuple-element.58.up_hbm, ...), custom_call_target="tpu_custom_call" | custom-call | tf_op jit(solution)/shard_map/cond/branch_1_fun/experts/pallas_call | solution.py:476
  189.8 14.4 %unpack.1 = bf16[4096,768]{1,0:T(8,128)(2,1)} custom-call(s32[32,128]{1,0:T(8,128)S(1)} %get-tuple-element.73.addr, s32[1,1]{1,0:T(1,128)} %get-tuple-element.74.flag, f32[32,128]{1,0:T(8,128)} %bitcast.5, bf16[8,49,16,768]{3,2,1,0:T(8,128)(2,1)} %get-tuple-element.76.back_hbm), custom_call_target="tpu_custom_call" | custom-call | tf_op jit(solution)/shard_map/unpack/pallas_call | solution.py:501

commit v6 on v5

--- a/solution.py
+++ b/solution.py
@@ -418,7 +418,7 @@
     if z is not None:
         hi = [min(hi[s], math.ceil(mean * (s + 1) + z * spread * math.sqrt(s + 1)), cap) for s in range(n_slot)]
         lo = [max(0, math.floor(mean * (s + 1) - z * spread * math.sqrt(s + 1))) for s in range(n_slot - 1)] + [0]
-    disp = [0, cap] if z is None else list(range(0, cap - CHUNK, CHUNK)) + [cap]
+    disp = [0, cap] if z is None else list(range(0, cap - CHUNK // 4, CHUNK)) + [cap]
     pieces = [(0, STEP, 0), (STEP, 2 * STEP, 0), (2 * STEP, disp[1], 0)]
     pieces += [(disp[j], disp[j + 1], j) for j in range(1, len(disp) - 1)]
     ret = [0] + [lo[s] // PACK * PACK for s in returns[:-1]] + [cap]
@@ -440,7 +440,7 @@
         mean = n_pairs // n_dev
         stride = up_to(n_slot * bound, PACK)
         caps = [min(stride, up_to(math.ceil(mean * f), PACK)) for f in TIERS]
-        cuts = [n_slot * c // 17 - 1 for c in (9, 12, 15, 17)]
+        cuts = [n_slot * c // 17 - 1 for c in (6, 9, 12, 15, 17)]
         plans = [plan(n_dev, n_slot, n_pairs, bound, stride, 4.0, c, cuts) for c in caps]
         plans.append(plan(n_dev, n_slot, n_pairs, bound, stride, None, stride, [n_slot - 1]))
         wide_bounds = plan(n_dev, n_slot, n_pairs, bound, stride, 4.0, stride, cuts)

time: 203 us -> 203 us (level)
  no operation moved by 1% of the time
where the time goes in v6:
time: 203 us
  Pallas kernels  201 us (99%)
    pallas_call x1, Pallas kernels, run(): pl.pallas_call(functools.partial(expert_kernel, cfg), out_shape=jax.Shape...  175 us
    pallas_call x1, Pallas kernels, group_layer(): pl.pallas_call(functools.partial(unpack_kernel, caps[-1], len(caps)), out...  14.4 us
    pallas_call x1, Pallas kernels, group_layer(): pl.pallas_call(functools.partial(route_kernel, n_dev, n_slot, stride, bou...  11.9 us

profile of v6, /device:TPU:113, one launch (start us, length us, event | category | flops | bytes accessed | tf_op | source)
XLA Modules:
  0.0 202.8 jit_solution(12318190996337819711)
XLA Ops:
  0.0 11.9 %route.1 = (s32[32,128]{1,0:T(8,128)S(1)}, s32[16,256]{1,0:T(8,128)S(1)}, s32[1,1]{1,0:T(1,128)}) custom-call(s32[32,128]{1,0:T(8,128)} %bitcast.6, s32[8,17]{1,0:T(8,128)} %table.1), custom_call_target="tpu_custom_call" | custom-call | tf_op jit(solution)/shard_map/route/pallas_call | solution.py:455
  12.6 175.6 %conditional.1 = (bf16[8,49,16,768]{3,2,1,0:T(8,128)(2,1)}) conditional(s32[]{:T(128)} %bitcast.2, (s32[16,256]{1,0:T(8,128)S(1)}, s32[32,128]{1,0:T(8,128)S(1)}, bf16[4096,768]{1,0:T(8,128)(2,1)}, bf16[17,768,3072]{2,1,0:T(8,128)(2,1)}, bf16[17,3072,768]{2,1,0:T(8,128)(2,1)}) %tuple.17, (s32[16,256]{1,0:T(8,128)S(1)}, ...), branch_computations={%region_0.0_spmd, %region_1.0_spmd, %region_2.0_spmd, %region_3.0_... | conditional | bytes 8 | solution.py:499
  12.6 174.8 %experts.4 = bf16[8,49,16,768]{3,2,1,0:T(8,128)(2,1)} custom-call(s32[16,256]{1,0:T(8,128)S(1)} %get-tuple-element.48.meta, s32[32,128]{1,0:T(8,128)S(1)} %get-tuple-element.50.addr, bf16[4096,768]{1,0:T(8,128)(2,1)} %get-tuple-element.52.tok_hbm, bf16[17,768,3072]{2,1,0:T(8,128)(2,1)} %get-tuple-element.53.up_hbm, ...), custom_call_target="tpu_custom_call" | custom-call | tf_op jit(solution)/shard_map/cond/branch_0_fun/experts/pallas_call | solution.py:476
  188.1 14.4 %unpack.1 = bf16[4096,768]{1,0:T(8,128)(2,1)} custom-call(s32[32,128]{1,0:T(8,128)S(1)} %get-tuple-element.73.addr, s32[1,1]{1,0:T(1,128)} %get-tuple-element.74.flag, f32[32,128]{1,0:T(8,128)} %bitcast.5, bf16[8,49,16,768]{3,2,1,0:T(8,128)(2,1)} %get-tuple-element.76.back_hbm), custom_call_target="tpu_custom_call" | custom-call | tf_op jit(solution)/shard_map/unpack/pallas_call | solution.py:501

commit v7 on v5

--- a/solution.py
+++ b/solution.py
@@ -229,16 +229,16 @@
 
     @pl.loop(0, n_rows)
     def _(r):
+        scale = jnp.broadcast_to(gate[pl.ds(r, 1), :], (LANES, n_col)).T
         for c in range(n_col // PACK):
             at = c * 2 * step
             for i in range(PACK):
                 a = addr[r, c * PACK + i]
-                g = gate[r, c * PACK + i]
-                tmp[pl.ds(at + (i // SUB) * step + i % SUB, d_tiles, stride=SUB), :] = wide[pl.ds(a, d_tiles, stride=SUB), :] * g
+                tmp[pl.ds(at + (i // SUB) * step + i % SUB, d_tiles, stride=SUB), :] = wide[pl.ds(a, d_tiles, stride=SUB), :]
             rows = pl.ds(pl.multiple_of(r * n_col + c * PACK, PACK), PACK)
             for j in range(d_tiles):
-                top = tmp[at + j * SUB:at + (j + 1) * SUB, :]
-                bot = tmp[at + step + j * SUB:at + step + (j + 1) * SUB, :]
+                top = tmp[at + j * SUB:at + (j + 1) * SUB, :] * scale[c * PACK:c * PACK + SUB]
+                bot = tmp[at + step + j * SUB:at + step + (j + 1) * SUB, :] * scale[c * PACK + SUB:(c + 1) * PACK]
                 out[rows, j * LANES:(j + 1) * LANES] = jnp.concatenate([top, bot], axis=0).astype(jnp.bfloat16)
         give(r).start()
 
@@ -417,7 +417,7 @@
     lo = [0] * n_slot
     if z is not None:
         hi = [min(hi[s], math.ceil(mean * (s + 1) + z * spread * math.sqrt(s + 1)), cap) for s in range(n_slot)]
-        lo = [max(0, math.floor(mean * (s + 1) - z * spread * math.sqrt(s + 1))) for s in range(n_slot - 1)] + [0]
+        lo = [max(0, math.floor(mean * (s + 1) - (z - 0.5) * spread * math.sqrt(s + 1))) if s in returns[:-1] else 0 for s in range(n_slot)]
     disp = [0, cap] if z is None else list(range(0, cap - CHUNK, CHUNK)) + [cap]
     pieces = [(0, STEP, 0), (STEP, 2 * STEP, 0), (2 * STEP, disp[1], 0)]
     pieces += [(disp[j], disp[j + 1], j) for j in range(1, len(disp) - 1)]
@@ -440,7 +440,7 @@
         mean = n_pairs // n_dev
         stride = up_to(n_slot * bound, PACK)
         caps = [min(stride, up_to(math.ceil(mean * f), PACK)) for f in TIERS]
-        cuts = [n_slot * c // 17 - 1 for c in (9, 12, 15, 17)]
+        cuts = [n_slot * c // 17 - 1 for c in (9, 12, 16, 17)]
         plans = [plan(n_dev, n_slot, n_pairs, bound, stride, 4.0, c, cuts) for c in caps]
         plans.append(plan(n_dev, n_slot, n_pairs, bound, stride, None, stride, [n_slot - 1]))
         wide_bounds = plan(n_dev, n_slot, n_pairs, bound, stride, 4.0, stride, cuts)
@@ -501,7 +501,7 @@
         return pl.pallas_call(
             functools.partial(unpack_kernel, caps[-1], len(caps)),
             out_shape=jax.ShapeDtypeStruct((n_tok, d_model), bf16),
-            in_specs=[smem, smem, smem, hbm],
+            in_specs=[smem, smem, vmem, hbm],
             out_specs=hbm,
             scratch_shapes=[block, wide, tmp, rows_vmem, sems, sem],
             compiler_params=pltpu.CompilerParams(vmem_limit_bytes=big),

time: 203 us -> 202 us (level); the launches traced: 204 us -> 200 us
  Pallas kernels: 203 us -> 198 us
    pallas_call x1, Pallas kernels: 177 us -> 173 us  [run(): pl.pallas_call(functools.partial(expert_kernel, cfg), out_shape=jax.Shape...]
where the time goes in v7:
time: 202 us; the launch traced here: 200 us
  Pallas kernels  198 us (98%)
    pallas_call x1, Pallas kernels, run(): pl.pallas_call(functools.partial(expert_kernel, cfg), out_shape=jax.Shape...  173 us
    pallas_call x1, Pallas kernels, group_layer(): pl.pallas_call(functools.partial(unpack_kernel, caps[-1], len(caps)), out...  13.2 us
    pallas_call x1, Pallas kernels, group_layer(): pl.pallas_call(functools.partial(route_kernel, n_dev, n_slot, stride, bou...  11.9 us

profile of v7, /device:TPU:113, one launch (start us, length us, event | category | flops | bytes accessed | tf_op | source)
XLA Modules:
  0.0 199.8 jit_solution(6761214251566714590)
XLA Ops:
  0.0 11.9 %route.1 = (s32[32,128]{1,0:T(8,128)S(1)}, s32[16,256]{1,0:T(8,128)S(1)}, s32[1,1]{1,0:T(1,128)}) custom-call(s32[32,128]{1,0:T(8,128)} %bitcast.6, s32[8,17]{1,0:T(8,128)} %table.1), custom_call_target="tpu_custom_call" | custom-call | tf_op jit(solution)/shard_map/route/pallas_call | solution.py:455
  12.6 173.8 %conditional.1 = (bf16[8,49,16,768]{3,2,1,0:T(8,128)(2,1)}) conditional(s32[]{:T(128)} %bitcast.2, (s32[16,256]{1,0:T(8,128)S(1)}, s32[32,128]{1,0:T(8,128)S(1)}, bf16[4096,768]{1,0:T(8,128)(2,1)}, bf16[17,768,3072]{2,1,0:T(8,128)(2,1)}, bf16[17,3072,768]{2,1,0:T(8,128)(2,1)}) %tuple.17, (s32[16,256]{1,0:T(8,128)S(1)}, ...), branch_computations={%region_0.0_spmd, %region_1.0_spmd, %region_2.0_spmd, %region_3.0_... | conditional | bytes 8 | solution.py:499
  12.6 173.0 %experts.4 = bf16[8,49,16,768]{3,2,1,0:T(8,128)(2,1)} custom-call(s32[16,256]{1,0:T(8,128)S(1)} %get-tuple-element.48.meta, s32[32,128]{1,0:T(8,128)S(1)} %get-tuple-element.50.addr, bf16[4096,768]{1,0:T(8,128)(2,1)} %get-tuple-element.52.tok_hbm, bf16[17,768,3072]{2,1,0:T(8,128)(2,1)} %get-tuple-element.53.up_hbm, ...), custom_call_target="tpu_custom_call" | custom-call | tf_op jit(solution)/shard_map/cond/branch_0_fun/experts/pallas_call | solution.py:476
  186.3 13.2 %unpack.1 = bf16[4096,768]{1,0:T(8,128)(2,1)} custom-call(s32[32,128]{1,0:T(8,128)S(1)} %get-tuple-element.73.addr, s32[1,1]{1,0:T(1,128)} %get-tuple-element.74.flag, f32[32,128]{1,0:T(8,128)} %bitcast.5, bf16[8,49,16,768]{3,2,1,0:T(8,128)(2,1)} %get-tuple-element.76.back_hbm), custom_call_target="tpu_custom_call" | custom-call | tf_op jit(solution)/shard_map/unpack/pallas_call | solution.py:501

commit v8 on v7

--- a/solution.py
+++ b/solution.py
@@ -440,7 +440,7 @@
         mean = n_pairs // n_dev
         stride = up_to(n_slot * bound, PACK)
         caps = [min(stride, up_to(math.ceil(mean * f), PACK)) for f in TIERS]
-        cuts = [n_slot * c // 17 - 1 for c in (9, 12, 16, 17)]
+        cuts = [n_slot * c // 17 - 1 for c in (9, 12, 14, 16, 17)]
         plans = [plan(n_dev, n_slot, n_pairs, bound, stride, 4.0, c, cuts) for c in caps]
         plans.append(plan(n_dev, n_slot, n_pairs, bound, stride, None, stride, [n_slot - 1]))
         wide_bounds = plan(n_dev, n_slot, n_pairs, bound, stride, 4.0, stride, cuts)

time: 202 us -> 199 us (0.985)
  Pallas kernels: 198 us -> 195 us
    pallas_call x1, Pallas kernels: 173 us -> 170 us  [run(): pl.pallas_call(functools.partial(expert_kernel, cfg), out_shape=jax.Shape...]
where the time goes in v8:
time: 199 us; the launch traced here: 197 us
  Pallas kernels  195 us (98%)
    pallas_call x1, Pallas kernels, run(): pl.pallas_call(functools.partial(expert_kernel, cfg), out_shape=jax.Shape...  170 us
    pallas_call x1, Pallas kernels, group_layer(): pl.pallas_call(functools.partial(unpack_kernel, caps[-1], len(caps)), out...  13.2 us
    pallas_call x1, Pallas kernels, group_layer(): pl.pallas_call(functools.partial(route_kernel, n_dev, n_slot, stride, bou...  11.9 us

profile of v8, /device:TPU:113, one launch (start us, length us, event | category | flops | bytes accessed | tf_op | source)
XLA Modules:
  0.0 196.6 jit_solution(11148953808352955431)
XLA Ops:
  0.0 11.9 %route.1 = (s32[32,128]{1,0:T(8,128)S(1)}, s32[16,256]{1,0:T(8,128)S(1)}, s32[1,1]{1,0:T(1,128)}) custom-call(s32[32,128]{1,0:T(8,128)} %bitcast.6, s32[8,17]{1,0:T(8,128)} %table.1), custom_call_target="tpu_custom_call" | custom-call | tf_op jit(solution)/shard_map/route/pallas_call | solution.py:455
  12.6 170.6 %conditional.1 = (bf16[8,49,16,768]{3,2,1,0:T(8,128)(2,1)}) conditional(s32[]{:T(128)} %bitcast.2, (s32[16,256]{1,0:T(8,128)S(1)}, s32[32,128]{1,0:T(8,128)S(1)}, bf16[4096,768]{1,0:T(8,128)(2,1)}, bf16[17,768,3072]{2,1,0:T(8,128)(2,1)}, bf16[17,3072,768]{2,1,0:T(8,128)(2,1)}) %tuple.17, (s32[16,256]{1,0:T(8,128)S(1)}, ...), branch_computations={%region_0.0_spmd, %region_1.0_spmd, %region_2.0_spmd, %region_3.0_... | conditional | bytes 8 | solution.py:499
  12.6 169.9 %experts.4 = bf16[8,49,16,768]{3,2,1,0:T(8,128)(2,1)} custom-call(s32[16,256]{1,0:T(8,128)S(1)} %get-tuple-element.48.meta, s32[32,128]{1,0:T(8,128)S(1)} %get-tuple-element.50.addr, bf16[4096,768]{1,0:T(8,128)(2,1)} %get-tuple-element.52.tok_hbm, bf16[17,768,3072]{2,1,0:T(8,128)(2,1)} %get-tuple-element.53.up_hbm, ...), custom_call_target="tpu_custom_call" | custom-call | tf_op jit(solution)/shard_map/cond/branch_0_fun/experts/pallas_call | solution.py:476
  183.2 13.2 %unpack.1 = bf16[4096,768]{1,0:T(8,128)(2,1)} custom-call(s32[32,128]{1,0:T(8,128)S(1)} %get-tuple-element.73.addr, s32[1,1]{1,0:T(1,128)} %get-tuple-element.74.flag, f32[32,128]{1,0:T(8,128)} %bitcast.5, bf16[8,49,16,768]{3,2,1,0:T(8,128)(2,1)} %get-tuple-element.76.back_hbm), custom_call_target="tpu_custom_call" | custom-call | tf_op jit(solution)/shard_map/unpack/pallas_call | solution.py:501
